TPU v7x, 32 devices: a 4x4x1 block of a 4x4x8 slice. The times are simulated.
32 devices in a mesh: pod: 1 (over z), d: 32 (over y, x, core).
Axes of the slice: x: 4, y: 4, z: 1, core: 2. Of those that a mesh axis runs over, the one named last changes fastest.
The devices are a block of a 4x4x8 slice.
Arguments:
- x: bfloat16 [32, 2048, 2048], P(('pod', 'd'))
- prompt_len: int32 [32], P(('pod', 'd'))
- ln_scale: float32 [2048], P('d')
- w_in: bfloat16 [2048, 18944], P('d')
- w_out: bfloat16 [10240, 2048], P(None, 'd')
Outputs:
- output 1: bfloat16 [32, 2048, 2048], P(('pod', 'd'))
- output 2: bfloat16 [32, 2048, 256], P(('pod', 'd'))
- output 3: bfloat16 [32, 2048, 256], P(('pod', 'd'))
All inputs are finite; a program needn't handle non-finite values.
Results may differ from a plain program's by a relative error of at most 0.00408039.
Values are sent between devices in bfloat16 or wider.
A program may use at most 768 MiB of HBM per device.

v0:
```python
import math
import jax
import jax.numpy as jnp
from jax import lax
from jax.sharding import PartitionSpec as P, NamedSharding

EPS = 1e-6
ROPE_BASE = 10000.0


def rope_tables(seq_len, head_dim):
    half_dim = head_dim // 2
    inv_freq = ROPE_BASE ** (-2.0 * jnp.arange(half_dim, dtype=jnp.float32) / head_dim)
    angles = jnp.arange(seq_len, dtype=jnp.float32)[:, None] * inv_freq[None, :]
    return jnp.cos(angles), jnp.sin(angles)


def apply_rope(rope_in, cos_b, sin_b):
    half_dim = rope_in.shape[-1] // 2
    lower_half = rope_in[..., :half_dim]
    upper_half = rope_in[..., half_dim:]
    return jnp.concatenate([lower_half * cos_b - upper_half * sin_b, upper_half * cos_b + lower_half * sin_b], axis=-1)


def layer_norm(x, ln_scale):
    x_float = x.astype(jnp.float32)
    centered = x_float - jnp.mean(x_float, axis=-1, keepdims=True)
    var_val = jnp.mean(centered * centered, axis=-1, keepdims=True)
    return (centered * lax.rsqrt(var_val + EPS) * ln_scale).astype(jnp.bfloat16)


def mix_tokens(projected, prompt_len, ffn_dim, attn_width, head_dim):
    num_seq = projected.shape[0]
    seq_len = projected.shape[1]
    num_heads = attn_width // head_dim
    q_start = 2 * ffn_dim
    k_start = q_start + attn_width
    v_start = k_start + head_dim
    gated = (jax.nn.silu(projected[..., :ffn_dim]) * projected[..., ffn_dim:q_start]).astype(jnp.bfloat16)
    cos_t, sin_t = rope_tables(seq_len, head_dim)
    q_rot = apply_rope(projected[..., q_start:k_start].reshape(num_seq, seq_len, num_heads, head_dim), cos_t[:, None, :], sin_t[:, None, :]).astype(jnp.bfloat16)
    k_rot = apply_rope(projected[..., k_start:v_start], cos_t, sin_t).astype(jnp.bfloat16)
    v_val = projected[..., v_start:].astype(jnp.bfloat16)
    scores = jnp.einsum("bthd,bsd->bths", q_rot, k_rot, preferred_element_type=jnp.float32) * (1.0 / math.sqrt(head_dim))
    positions = jnp.arange(seq_len)
    causal = positions[None, :] <= positions[:, None]
    valid_key = positions[None, :] < prompt_len[:, None]
    allowed = causal[None, :, None, :] & valid_key[:, None, None, :]
    probs_bf = jax.nn.softmax(jnp.where(allowed, scores, -1e30), axis=-1).astype(jnp.bfloat16)
    attn_out = jnp.einsum("bths,bsd->bthd", probs_bf, v_val, preferred_element_type=jnp.float32).astype(jnp.bfloat16)
    return gated, attn_out.reshape(num_seq, seq_len, attn_width), k_rot, v_val


def layer_math(x, prompt_len, ln_scale, w_in, w_out):
    model_width = x.shape[2]
    ffn_dim = 4 * model_width
    attn_width = w_out.shape[0] - ffn_dim
    head_dim = (w_in.shape[1] - 2 * ffn_dim - attn_width) // 2
    h_norm = layer_norm(x, ln_scale)
    projected = jnp.einsum("bte,ec->btc", h_norm, w_in, preferred_element_type=jnp.float32)
    gated, attn_out, k_rot, v_val = mix_tokens(projected, prompt_len, ffn_dim, attn_width, head_dim)
    out_sum = (jnp.einsum("btf,fe->bte", gated, w_out[:ffn_dim], preferred_element_type=jnp.float32)
               + jnp.einsum("btf,fe->bte", attn_out, w_out[ffn_dim:], preferred_element_type=jnp.float32))
    y_out = (x.astype(jnp.float32) + out_sum).astype(jnp.bfloat16)
    return y_out, k_rot, v_val


def solution(mesh):
    batch_spec = P(("pod", "d"))

    def local_layer(x, prompt_len, ln_shard, w_in_shard, w_out_shard):
        ln_scale = lax.all_gather(ln_shard, "d", axis=0, tiled=True)
        w_in = lax.all_gather(w_in_shard, "d", axis=0, tiled=True)
        w_out = lax.all_gather(w_out_shard, "d", axis=1, tiled=True)
        return layer_math(x, prompt_len, ln_scale, w_in, w_out)

    return jax.shard_map(local_layer, mesh=mesh,
                         in_specs=(batch_spec, batch_spec, P("d"), P("d", None), P(None, "d")),
                         out_specs=(batch_spec, batch_spec, batch_spec), check_vma=False)
```

profile of v0, /device:TPU:96, one launch (start us, length us, event | category | flops | bytes accessed | tf_op | source)
XLA Modules:
  0.0 685.3 jit_solution(16744884983874212336)
XLA Ops:
  7.2 0.1 all-gather.3.cloned.1.call-start
  7.2 0.7 all-gather.3.cloned.1.call-update
  8.0 0.1 all-gather.5.cloned.1.call-start
  8.0 0.7 all-gather.5.cloned.1.call-update
  9.4 0.9 dynamic-update-slice
  10.3 50.5 %all-reduce = f32[2048]{0:T(1024)S(1)} all-reduce(f32[2048]{0:T(1024)S(1)} %dynamic-update-slice), channel_id=1, replica_groups=mesh['pod'=1,'d'=32] {'d'}, use_global_device_ids=true, to_apply=%add | all-reduce | flops 2048 | bytes 16384
  60.8 0.0 copy-start.4
  60.8 4.5 convert_reduce_fusion
  65.4 5.7 fusion.13
  71.1 0.0 copy-done.4
  71.1 4.8 fusion.34
  75.9 5.1 fusion.17
  81.0 155.5 %all-gather.3.cloned.1.call-done = bf16[2048,18944]{1,0:T(8,128)(2,1)} async-done(((bf16[64,18944]{1,0:T(8,128)(2,1)}), bf16[2048,18944]{1,0:T(8,128)(2,1)}) %all-gather.3.cloned.1.call-update) | async-done | bytes 77594640 | tf_op jit(solution)/shard_map/all_gather | solution.py:73
  236.5 185.3 %convolution_bitcast_fusion = f32[1,2048,18944]{2,1,0:T(8,128)} fusion(bf16[2048,18944]{1,0:T(8,128)(2,1)} %all-gather.3.cloned.1.call-done, bf16[1,2048,2048]{2,1,0:T(8,128)(2,1)} %param.5, f32[2048]{0:T(1024)S(1)} %all-reduce, f32[2048]{0:T(1024)S(1)} %add_rsqrt_fusion, f32[2048]{0:T(1024)S(1)} %broadcast_multiply_fusion), kind=kOutput, calls=%fused_computation.5 | convolution fusion | flops 158934761472 | bytes 241197056 | tf_op jit(solution)/shard_map/bte,ec->btc/dot_general | solution.py:60
  421.7 1.7 slice.73
  423.4 0.0 copy-start.3
  423.4 0.0 slice-start
  423.5 6.1 slice-done
  429.6 0.0 copy-start.5
  429.6 6.0 copy.17
  435.6 0.0 copy-done.5
  435.6 5.5 subtract_convert_fusion.1
  441.2 1.1 pad_maximum_fusion.7
  442.2 0.0 copy-start.1
  442.2 0.0 copy-start.2
  442.3 6.4 fusion.42
  448.7 0.0 copy-done.1
  448.7 0.0 copy-done.2
  448.7 11.9 %fusion.28 = (bf16[2048,8,128]{2,0,1:T(8,128)(2,1)}, bf16[2048,8,128]{2,0,1:T(8,128)(2,1)}) fusion(f32[1,2048,8,128]{3,2,1,0:T(8,128)} %get-tuple-element.7, f32[1,2048,8,128]{3,2,1,0:T(8,128)} %get-tuple-element.8, f32[2048,128]{1,0:T(8,128)S(1)} %copy-done.2, f32[2048,128]{1,0:T(8,128)S(1)} %copy-done.1), kind=kLoop, calls=%fused_computation.37 | loop fusion | flops 16777216 | bytes 27262976 | tf_op jit(solution)/shard_map/concatenate | solution.py:22
  460.6 53.0 %fusion.43 = (f32[2048,8]{0,1:T(8,128)S(1)}, f32[2048,8,2048]{0,2,1:T(8,128)}) fusion(pred[2048,2048]{0,1:T(8,128)(4,1)} %fusion.17, bf16[2048,8,128]{2,0,1:T(8,128)(2,1)} %get-tuple-element.6, bf16[2048,8,128]{2,0,1:T(8,128)(2,1)} %get-tuple-element.5, bf16[2048,128]{1,0:T(8,128)(2,1)S(1)} %bitcast.50, bf16[2048,128]{1,0:T(8,128)(2,1)S(1)} %bitcast.49), kind=kOutput, calls=%fused_computation.61 | convolution fusion | flops 17332963328 | bytes 147914752 | tf_op jit(solution)/shard_map/sub | solution.py:49
  513.5 0.0 copy-done.3
  513.5 51.7 %fusion.27 = bf16[2048,8,256]{0,2,1:T(8,128)(2,1)} fusion(f32[2048,8,2048]{0,2,1:T(8,128)} %get-tuple-element.12, f32[2048,8]{0,1:T(8,128)S(1)} %get-tuple-element.11, bf16[1,2048,256]{2,1,0:T(8,128)(2,1)S(1)} %slice.73), kind=kOutput, calls=%fused_computation.36 | convolution fusion | flops 17251172352 | bytes 143720448 | tf_op jit(solution)/shard_map/bths,bsd->bthd/dot_general | solution.py:50
  565.2 0.0 all-gather.5.cloned.1.call-done
  565.2 0.0 copy-start
  565.2 86.5 %fusion.7 = f32[2048,2048]{1,0:T(8,128)} fusion(bf16[10240,2048]{0,1:T(8,128)(2,1)} %all-gather.5.cloned.1.call-done, f32[1,2048,18944]{2,1,0:T(8,128)} %convolution_bitcast_fusion), kind=kOutput, calls=%fused_computation.12 | convolution fusion | flops 68820140032 | bytes 184549376 | tf_op jit(solution)/shard_map/btf,fe->bte/dot_general | solution.py:62
  651.7 0.0 copy-done
  651.7 26.3 %fusion.16 = bf16[1,2048,2048]{2,1,0:T(8,128)(2,1)} fusion(bf16[1,2048,2048]{2,1,0:T(8,128)(2,1)S(1)} %copy-done, f32[2048,2048]{1,0:T(8,128)} %fusion.7, bf16[2048,2048]{0,1:T(8,128)(2,1)} %bitcast.51, bf16[10240,2048]{0,1:T(8,128)(2,1)} %all-gather.5.cloned.1.call-done), kind=kOutput, calls=%fused_computation.23 | convolution fusion | flops 17196646400 | bytes 50331648 | tf_op jit(solution)/shard_map/btf,fe->bte/dot_general | solution.py:63
  (5 shorter events, 0.0 us)
Async XLA Ops:
  7.2 229.3 %all-gather.3.cloned.1.call-start = ((), (), s32[]{:S(2)}) async-start(), calls=%async_computation | async-start | bytes 80019456 | tf_op jit(solution)/shard_map/all_gather | solution.py:73
  8.0 557.2 %all-gather.5.cloned.1.call-start = ((), (), s32[]{:S(2)}) async-start(), calls=%async_computation.1 | async-start | bytes 43253760 | tf_op jit(solution)/shard_map/all_gather | solution.py:74
  60.8 10.3 %copy-start.4 = (f32[128]{0:T(128)}, f32[128]{0:T(128)S(1)}, u32[]{:S(2)}) copy-start(f32[128]{0:T(128)S(1)} %multiply_power_fusion) | copy-start | bytes 1540
  423.4 90.1 %copy-start.3 = (bf16[1,2048,256]{2,1,0:T(8,128)(2,1)}, bf16[1,2048,256]{2,1,0:T(8,128)(2,1)S(1)}, u32[]{:S(2)}) copy-start(bf16[1,2048,256]{2,1,0:T(8,128)(2,1)S(1)} %slice.73) | copy-start | bytes 3145732
  423.4 6.1 slice-start
  429.6 6.0 copy-start.5
  442.2 6.4 copy-start.1
  442.2 6.4 copy-start.2
  565.2 86.5 %copy-start = (bf16[1,2048,2048]{2,1,0:T(8,128)(2,1)S(1)}, bf16[1,2048,2048]{2,1,0:T(8,128)(2,1)}, u32[]{:S(2)}) copy-start(bf16[1,2048,2048]{2,1,0:T(8,128)(2,1)} %param.5) | copy-start | bytes 25165828
Sparse Core Ops, SparseCore 0:
  10.1 226.3 all-gather.2
  238.5 129.3 all-gather.4
where the time goes:
time: 693 us; the launch traced here: 685 us
  matrix products  403 us (58%)
  waiting for transfers between devices  157 us (23%)
  blocking collectives  50.5 us (7%)
  other arithmetic  38.6 us (6%)
  local copies, waits for them, and re-layouts  21.2 us (3%)
  between operations  15.3 us (2%)
    dot_general x1, matrix products, layer_math(): jnp.einsum('bte,ec->btc', h_norm, w_in, preferred_element_type=jnp.float32)  185 us
    all_gather x1, waiting for transfers between devices, local_layer(): w_in = lax.all_gather(w_in_shard, 'd', axis=0, tiled=True)  156 us
    dot_general x1, matrix products, layer_math(): jnp.einsum('btf,fe->bte', gated, w_out[:ffn_dim], preferred_element_type=...  86.5 us
    sub x1, matrix products, mix_tokens(): jax.nn.softmax(jnp.where(allowed, scores, -1e+30), axis=-1)  53 us
    dot_general x1, matrix products, mix_tokens(): jnp.einsum('bths,bsd->bthd', probs_bf, v_val, preferred_element_type=jnp....  51.7 us
    unnamed x1, blocking collectives  50.5 us
    dot_general x1, matrix products, layer_math(): jnp.einsum('btf,fe->bte', attn_out, w_out[ffn_dim:], preferred_element_ty...  26.3 us
  transfers between devices with their start and end apart: 2, of which 1 were waited for; matrix products, arithmetic and copies ran while one was open for 50% of the time, Pallas kernels for 0%

commit v1 on v0

v1 whole, which is shorter than its diff:
```python
import functools
import math

import jax
import jax.numpy as jnp
import numpy as np
from jax import lax
from jax.experimental import pallas as pl
from jax.experimental.pallas import tpu as pltpu
from jax.sharding import PartitionSpec as P

EPS = 1e-6
ROPE_BASE = 10000.0
MASKED = -1e30
MESH = pl.DeviceIdType.MESH
HBM = pltpu.HBM
VMEM_LIMIT = 67043328

CHUNK = 384
LAG = (0, 2, 4, 6, 8, 10)


def dims(mesh, x, w_in, w_out):
    devices = mesh.shape["d"]
    cores = 2
    side = math.isqrt(devices // cores)
    model = x.shape[2]
    ffn = 4 * model
    attn = w_out.shape[0] - ffn
    head = (w_in.shape[1] - 2 * ffn - attn) // 2
    return dict(D=devices, CORES=cores, SIDE=side, T=x.shape[1], E=model, F=ffn, H=attn // head, HD=head,
                R=model // devices, COLS=w_in.shape[1] + w_out.shape[0], FC=head)


def rope_tables(seq_len, head_dim):
    half = head_dim // 2
    inv_freq = np.float32(ROPE_BASE) ** (np.float32(-2.0) * np.arange(half, dtype=np.float32) / np.float32(head_dim))
    return inv_freq


def place():
    return lax.axis_index("d")


def order_copies(d, win_ref, wot_ref, stage_ref, sem):
    F, H, HD, FC = d["F"], d["H"], d["HD"], d["FC"]
    qs = 2 * F
    ks = qs + H * HD
    pltpu.make_async_copy(win_ref.at[:, pl.ds(ks, 2 * HD)], stage_ref.at[:, pl.ds(0, 2 * HD)], sem).start()

    @pl.loop(0, H)
    def _(h):
        at = pl.multiple_of(2 * HD + h * 2 * HD, HD)
        pltpu.make_async_copy(win_ref.at[:, pl.ds(pl.multiple_of(qs + h * HD, HD), HD)],
                              stage_ref.at[:, pl.ds(at, HD)], sem).start()
        pltpu.make_async_copy(wot_ref.at[:, pl.ds(pl.multiple_of(F + h * HD, HD), HD)],
                              stage_ref.at[:, pl.ds(at + HD, HD)], sem).start()

    base = 2 * HD + H * 2 * HD

    @pl.loop(0, F // FC)
    def _(j):
        at = pl.multiple_of(base + j * 3 * FC, FC)
        pltpu.make_async_copy(win_ref.at[:, pl.ds(pl.multiple_of(j * FC, FC), FC)],
                              stage_ref.at[:, pl.ds(at, FC)], sem).start()
        pltpu.make_async_copy(win_ref.at[:, pl.ds(pl.multiple_of(F + j * FC, FC), FC)],
                              stage_ref.at[:, pl.ds(at + FC, FC)], sem).start()
        pltpu.make_async_copy(wot_ref.at[:, pl.ds(pl.multiple_of(j * FC, FC), FC)],
                              stage_ref.at[:, pl.ds(at + 2 * FC, FC)], sem).start()


class Comm:
    def __init__(self, d, stage_ref, w_ref, send_sem, recv_sem):
        self.d = d
        self.stage, self.w, self.send, self.recv = stage_ref, w_ref, send_sem, recv_sem
        self.groups = d["COLS"] // CHUNK
        side, cores = d["SIDE"], d["CORES"]
        me = place()
        self.me = me
        self.core = lax.rem(me, cores)
        self.x = lax.rem(lax.div(me, cores), side)
        self.y = lax.div(me, cores * side)

    def dev(self, y, x, core):
        d = self.d
        return {"d": (y * d["SIDE"] + x) * d["CORES"] + core}

    def wrap(self, v):
        side = self.d["SIDE"]
        return lax.rem(v + side, side)

    def put(self, src, dst, stage, g, device):
        return pltpu.make_async_remote_copy(src_ref=src, dst_ref=dst, send_sem=self.send.at[stage],
                                            recv_sem=self.recv.at[stage, g], device_id=device, device_id_type=MESH)

    def landed(self, ref, stage, g):
        pltpu.make_async_copy(ref, ref, self.recv.at[stage, g]).wait()

    def stage_fn(self, stage, g):
        w, x, y, c = self.w, self.x, self.y, self.core
        half = self.d["R"] // 2
        cols = pl.ds(pl.multiple_of(g * CHUNK, 128), CHUNK)
        ra, rb = pl.ds(0, half), pl.ds(half, half)
        turn = 1 - 2 * lax.rem(g, 2)
        if stage == 0:
            for s in (1, -1):
                self.put(self.stage.at[ra, cols], w.at[y, x, c, ra, cols], 0, g,
                         self.dev(y, self.wrap(x + s), c)).start()
                self.put(self.stage.at[rb, cols], w.at[y, x, c, rb, cols], 0, g,
                         self.dev(self.wrap(y + s), x, c)).start()
        elif stage == 1:
            self.landed(w.at[0, 0:2, :, ra, cols], 0, g)
            xs, ys = self.wrap(x - turn), self.wrap(y + turn)
            a = w.at[y, xs, c, ra, cols]
            self.put(a, a, 1, g, self.dev(y, self.wrap(x + turn), c)).start()
            b = w.at[ys, x, c, rb, cols]
            self.put(b, b, 1, g, self.dev(self.wrap(y - turn), x, c)).start()
        elif stage == 2:
            self.landed(w.at[0, 0, :, ra, cols], 1, g)
            a = w.at[y, :, c, ra, cols]
            b = w.at[:, x, c, rb, cols]
            for s in (1, -1):
                self.put(a, a, 2, g, self.dev(self.wrap(y + s), x, c)).start()
                self.put(b, b, 2, g, self.dev(y, self.wrap(x + s), c)).start()
        elif stage == 3:
            self.landed(w.at[0:2, :, :, ra, cols], 2, g)
            ys, xs = self.wrap(y - turn), self.wrap(x + turn)
            a = w.at[ys, :, c, ra, cols]
            self.put(a, a, 3, g, self.dev(self.wrap(y + turn), x, c)).start()
            b = w.at[:, xs, c, rb, cols]
            self.put(b, b, 3, g, self.dev(y, self.wrap(x - turn), c)).start()
        elif stage == 4:
            self.landed(w.at[0, :, :, ra, cols], 3, g)
            a = w.at[:, :, c, :, cols]
            self.put(a, a, 4, g, self.dev(y, x, 1 - c)).start()
        else:
            self.landed(w.at[:, :, 0, :, cols], 4, g)

    def point(self, p):
        for stage in range(6):
            g = p - LAG[stage]
            if isinstance(g, int):
                if 0 <= g < self.groups:
                    self.stage_fn(stage, g)
            else:
                @pl.when(jnp.logical_and(g >= 0, g < self.groups))
                def _(stage=stage, g=g):
                    self.stage_fn(stage, g)

    def drain(self):
        side, w = self.d["SIDE"], self.w
        for stage, ref in ((0, w.at[0, 0]), (1, w.at[0, 0, 0]), (2, w.at[0]), (3, w.at[0, 0:side // 2]),
                           (4, w.at[0:side // 2])):
            pltpu.make_async_copy(ref, ref, self.send.at[stage]).wait()


def meet(d):
    barrier = pltpu.get_barrier_semaphore()
    me = place()

    @pl.loop(1, d["D"])
    def _(i):
        pl.semaphore_signal(barrier, inc=1, device_id={"d": lax.rem(me + i, d["D"])}, device_id_type=MESH)

    pl.semaphore_wait(barrier, d["D"] - 1)


def spread_scale(d, ln_ref, ln_all, ln_send, ln_recv):
    me = place()

    @pl.loop(1, d["D"])
    def _(i):
        pltpu.make_async_remote_copy(src_ref=ln_ref, dst_ref=ln_all.at[me], send_sem=ln_send, recv_sem=ln_recv,
                                     device_id={"d": lax.rem(me + i, d["D"])}, device_id_type=MESH).start()

    ln_all[me] = ln_ref[...]


def spread_scale_wait(d, ln_all, ln_send, ln_recv):
    rest = ln_all.at[pl.ds(0, d["D"] - 1)]
    pltpu.make_async_copy(rest, rest, ln_recv).wait()
    pltpu.make_async_copy(rest, rest, ln_send).wait()


def scale_row(d, ln_all, row_ref):
    lane = lax.broadcasted_iota(jnp.int32, (1, 128), 1)
    per = 128 // d["R"]
    for i in range(d["E"] // 128):
        part = ln_all[per * i][0:1, :]
        for k in range(1, per):
            part = jnp.where(lane < k * d["R"], part, ln_all[per * i + k][0:1, :])
        row_ref[0:1, i * 128:(i + 1) * 128] = part


def gather_kernel(d, ln_ref, win_ref, wot_ref, w_ref, lnout_ref, stage_ref, ln_all, local_sem, ln_send, ln_recv,
                  send_sem, recv_sem):
    order_copies(d, win_ref, wot_ref, stage_ref, local_sem.at[0])
    comm = Comm(d, stage_ref, w_ref, send_sem, recv_sem)
    own = pltpu.make_async_copy(stage_ref, w_ref.at[comm.y, comm.x, comm.core], local_sem.at[1])
    meet(d)
    spread_scale(d, ln_ref, ln_all, ln_send, ln_recv)
    pltpu.make_async_copy(stage_ref, stage_ref, local_sem.at[0]).wait()
    own.start()
    spread_scale_wait(d, ln_all, ln_send, ln_recv)
    comm.point(0)
    comm.point(1)
    own.wait()

    @pl.loop(2, comm.groups + LAG[5])
    def _(p):
        comm.point(p)

    comm.drain()
    scale_row(d, ln_all, lnout_ref)


def gather(d, mesh, ln, w_in, wot):
    groups = d["COLS"] // CHUNK
    ln_tile = jnp.broadcast_to(jnp.tile(ln, 128 // d["R"])[None], (8, 128))
    w_shape = (d["SIDE"], d["SIDE"], d["CORES"], d["R"], d["COLS"])
    return pl.pallas_call(
        functools.partial(gather_kernel, d),
        out_shape=(jax.ShapeDtypeStruct(w_shape, jnp.bfloat16), jax.ShapeDtypeStruct((1, d["E"]), jnp.float32)),
        in_specs=[pl.BlockSpec(memory_space=pltpu.VMEM), pl.BlockSpec(memory_space=HBM), pl.BlockSpec(memory_space=HBM)],
        out_specs=(pl.BlockSpec(memory_space=HBM), pl.BlockSpec(memory_space=pltpu.VMEM)),
        scratch_shapes=[
            pltpu.VMEM((d["R"], d["COLS"]), jnp.bfloat16),
            pltpu.VMEM((d["D"], 8, 128), jnp.float32),
            pltpu.SemaphoreType.DMA((2,)),
            pltpu.SemaphoreType.DMA,
            pltpu.SemaphoreType.DMA,
            pltpu.SemaphoreType.DMA((5,)),
            pltpu.SemaphoreType.DMA((5, groups)),
        ],
        compiler_params=pltpu.CompilerParams(collective_id=0, has_side_effects=True, vmem_limit_bytes=VMEM_LIMIT),
        name="gather",
    )(ln_tile, w_in, wot)


def nn(a, b):
    return lax.dot_general(a, b, (((1,), (0,)), ((), ())), preferred_element_type=jnp.float32)


def nt(a, b):
    return lax.dot_general(a, b, (((1,), (1,)), ((), ())), preferred_element_type=jnp.float32)


def rope(u, cos, sin):
    half = u.shape[1] // 2
    u1, u2 = u[:, :half], u[:, half:]
    return jnp.concatenate([u1 * cos - u2 * sin, u2 * cos + u1 * sin], axis=1)


class Layer:
    XB = 128
    MB = 512
    QB = 256

    def __init__(self, d, r):
        self.d, self.r = d, r

    def x_copy(self, i, slot):
        rows = pl.ds(pl.multiple_of(i * self.XB, self.XB), self.XB)
        return pltpu.make_async_copy(self.r.x.at[0, rows, :], self.r.xbuf.at[slot], self.r.xsem.at[slot])

    def unit(self, col, buf, sem):
        return pltpu.make_async_copy(self.r.w.at[:, :, :, :, pl.ds(pl.multiple_of(col, 128), self.d["FC"])], buf, sem)

    def wval(self, buf):
        return buf[...].reshape(self.d["E"], self.d["FC"])

    def norm(self):
        d, r = self.d, self.r
        n = d["T"] // self.XB
        self.x_copy(0, 0).start()

        @pl.loop(0, n)
        def _(i):
            slot = lax.rem(i, 2)

            @pl.when(i + 1 < n)
            def _():
                self.x_copy(i + 1, 1 - slot).start()

            self.x_copy(i, slot).wait()
            rows = pl.ds(pl.multiple_of(i * self.XB, self.XB), self.XB)
            xf = r.xbuf[slot].astype(jnp.float32)
            centered = xf - jnp.mean(xf, axis=-1, keepdims=True)
            var = jnp.mean(centered * centered, axis=-1, keepdims=True)
            r.h[rows, :] = (centered * lax.rsqrt(var + EPS) * r.ln[...]).astype(jnp.bfloat16)
            r.yacc[rows, :] = xf

    def tables(self):
        d, r = self.d, self.r
        lo = r.rc.shape[0] - d["T"] // self.QB
        cl, sl = r.rc[0:self.QB, :], r.rs[0:self.QB, :]
        for b in range(d["T"] // self.QB):
            cb, sb = r.rc[self.QB + b:self.QB + b + 1, :], r.rs[self.QB + b:self.QB + b + 1, :]
            rows = slice(b * self.QB, (b + 1) * self.QB)
            r.cos[rows, :] = cl * cb - sl * sb
            r.sin[rows, :] = sl * cb + cl * sb

    def bias(self):
        r, d = self.r, self.d
        col = lax.broadcasted_iota(jnp.int32, (8, d["T"]), 1)
        r.bias[...] = jnp.where(col < r.plen[0], 0.0, MASKED)

    def keys(self, kbuf, vbuf):
        r, d = self.r, self.d
        for m in range(d["T"] // self.MB):
            rows = slice(m * self.MB, (m + 1) * self.MB)
            hb = r.h[rows, :]
            r.k[rows, :] = rope(nn(hb, self.wval(kbuf)), r.cos[rows, :], r.sin[rows, :]).astype(jnp.bfloat16)
            r.v[rows, :] = nn(hb, self.wval(vbuf)).astype(jnp.bfloat16)

    def query(self, qbuf):
        r, d = self.r, self.d
        scale = 1.0 / math.sqrt(d["HD"])
        for m in range(d["T"] // self.MB):
            rows = slice(m * self.MB, (m + 1) * self.MB)
            q = rope(nn(r.h[rows, :], self.wval(qbuf)), r.cos[rows, :], r.sin[rows, :]).astype(jnp.bfloat16)
            r.q[rows, :] = q * jnp.bfloat16(scale)

    def attend(self):
        r, d = self.r, self.d
        qb = self.QB
        row = lax.broadcasted_iota(jnp.int32, (qb, qb), 0)
        col = lax.broadcasted_iota(jnp.int32, (qb, qb), 1)
        for b in range(d["T"] // qb):
            n = (b + 1) * qb
            rows = slice(b * qb, n)
            s = nt(r.q[rows, :], r.k[0:n, :]) + r.bias[0:1, 0:n]
            last = jnp.where(col <= row, s[:, n - qb:], MASKED)
            s = last if b == 0 else jnp.concatenate([s[:, :n - qb], last], axis=1)
            e = jnp.exp(s - jnp.max(s, axis=-1, keepdims=True))
            p = (e * (1.0 / jnp.sum(e, axis=-1, keepdims=True))).astype(jnp.bfloat16)
            r.o[rows, :] = nn(p, r.v[0:n, :]).astype(jnp.bfloat16)

    def add_out(self, a_ref, obuf, tile):
        r, d = self.r, self.d
        fc = d["FC"]
        per = fc // d["R"]
        cols = slice(tile * fc, (tile + 1) * fc)
        w = self.wval(obuf)[cols, :]
        r.yacc[:, cols] += nt(a_ref[...], w)

    def gated(self, m, gbuf, ubuf, a_ref):
        r = self.r
        rows = slice(m * self.MB, (m + 1) * self.MB)
        hb = r.h[rows, :]
        g = nn(hb, self.wval(gbuf))
        u = nn(hb, self.wval(ubuf))
        hg = g * 0.5
        a_ref[rows, :] = ((hg + hg * jnp.tanh(hg)) * u).astype(jnp.bfloat16)

    def finish(self):
        d, r = self.d, self.r
        n = d["T"] // self.XB

        def out(i, slot):
            rows = pl.ds(pl.multiple_of(i * self.XB, self.XB), self.XB)
            return pltpu.make_async_copy(r.xbuf.at[slot], r.y.at[0, rows, :], r.xsem.at[slot])

        @pl.loop(0, n)
        def _(i):
            slot = lax.rem(i, 2)

            @pl.when(i >= 2)
            def _():
                out(i - 2, slot).wait()

            rows = pl.ds(pl.multiple_of(i * self.XB, self.XB), self.XB)
            r.xbuf[slot] = r.yacc[rows, :].astype(jnp.bfloat16)
            out(i, slot).start()

        out(n - 2, n % 2).wait()
        out(n - 1, 1 - n % 2).wait()


class Refs:
    pass


LAYER_NAMES = ("x", "plen", "ln", "rc", "rs", "w", "y", "kc", "vc", "h", "yacc", "xbuf", "cos", "sin", "bias", "k", "v", "q", "o", "a",
               "wbuf", "obuf", "xsem", "wsem", "osem", "csem")


def layer_scratch(d):
    T, E, HD, FC = d["T"], d["E"], d["HD"], d["FC"]
    unit = (d["SIDE"], d["SIDE"], d["CORES"], d["R"], FC)
    return [
        pltpu.VMEM((T, E), jnp.bfloat16),
        pltpu.VMEM((T, E), jnp.float32),
        pltpu.VMEM((2, Layer.XB, E), jnp.bfloat16),
        pltpu.VMEM((T, HD // 2), jnp.float32),
        pltpu.VMEM((T, HD // 2), jnp.float32),
        pltpu.VMEM((8, T), jnp.float32),
        pltpu.VMEM((T, HD), jnp.bfloat16),
        pltpu.VMEM((T, HD), jnp.bfloat16),
        pltpu.VMEM((T, HD), jnp.bfloat16),
        pltpu.VMEM((T, HD), jnp.bfloat16),
        pltpu.VMEM((2, T, FC), jnp.bfloat16),
        pltpu.VMEM((2, 2) + unit, jnp.bfloat16),
        pltpu.VMEM((3,) + unit, jnp.bfloat16),
        pltpu.SemaphoreType.DMA((2,)),
        pltpu.SemaphoreType.DMA((2, 2)),
        pltpu.SemaphoreType.DMA((3,)),
        pltpu.SemaphoreType.DMA((2,)),
    ]


def layer_kernel(d, *refs):
    r = Refs()
    for name, ref in zip(LAYER_NAMES, refs, strict=True):
        setattr(r, name, ref)
    L = Layer(d, r)
    HD, FC, H = d["HD"], d["FC"], d["H"]
    J = d["F"] // FC
    tiles = d["E"] // FC
    mbs = d["T"] // L.MB
    base = 2 * HD + H * 2 * HD

    def fetch_kv():
        return [L.unit(0, r.wbuf.at[0, 0], r.wsem.at[0, 0]), L.unit(HD, r.wbuf.at[0, 1], r.wsem.at[0, 1])]

    def fetch_head(h):
        col = 2 * HD + h * 2 * HD
        return [L.unit(col, r.wbuf.at[1, lax.rem(h, 2)], r.wsem.at[1, lax.rem(h, 2)]),
                L.unit(col + HD, r.obuf.at[lax.rem(h, 2)], r.osem.at[lax.rem(h, 2)])]

    def fetch_mlp(j):
        col = base + j * 3 * FC
        s = lax.rem(j, 2)
        o = lax.rem(j, 3)
        return [L.unit(col, r.wbuf.at[s, 0], r.wsem.at[s, 0]), L.unit(col + FC, r.wbuf.at[s, 1], r.wsem.at[s, 1]),
                L.unit(col + 2 * FC, r.obuf.at[o], r.osem.at[o])]

    def start(copies):
        for c in copies:
            c.start()

    def wait(copies):
        for c in copies:
            c.wait()

    start(fetch_kv())
    start(fetch_head(0))
    L.norm()
    L.tables()
    L.bias()
    wait(fetch_kv())
    L.keys(r.wbuf.at[0, 0], r.wbuf.at[0, 1])
    pltpu.make_async_copy(r.k, r.kc.at[0], r.csem.at[0]).start()
    pltpu.make_async_copy(r.v, r.vc.at[0], r.csem.at[1]).start()

    @pl.loop(0, H)
    def _(h):
        @pl.when(h + 1 < H)
        def _():
            start(fetch_head(h + 1))

        wait(fetch_head(h))
        L.query(r.wbuf.at[1, lax.rem(h, 2)])
        L.attend()
        for t in range(tiles):
            L.add_out(r.o, r.obuf.at[lax.rem(h, 2)], t)

    start(fetch_mlp(0))
    start(fetch_mlp(1))

    wait(fetch_mlp(0))
    for m in range(mbs):
        L.gated(m, r.wbuf.at[0, 0], r.wbuf.at[0, 1], r.a.at[0])

    @pl.loop(1, J)
    def _(j):
        @pl.when(j + 1 < J)
        def _():
            start(fetch_mlp(j + 1))

        wait(fetch_mlp(j))
        s = lax.rem(j, 2)
        prev = r.obuf.at[lax.rem(j - 1, 3)]
        per = tiles // mbs
        for m in range(mbs):
            L.gated(m, r.wbuf.at[s, 0], r.wbuf.at[s, 1], r.a.at[s])
            for t in range(m * per, (m + 1) * per):
                L.add_out(r.a.at[1 - s], prev, t)

    for t in range(tiles):
        L.add_out(r.a.at[(J - 1) % 2], r.obuf.at[(J - 1) % 3], t)
    L.finish()
    pltpu.make_async_copy(r.k, r.kc.at[0], r.csem.at[0]).wait()
    pltpu.make_async_copy(r.v, r.vc.at[0], r.csem.at[1]).wait()


def layer(d, x, prompt_len, ln_row, w):
    T, E, HD = d["T"], d["E"], d["HD"]
    half = HD // 2
    inv_freq = np.float64(ROPE_BASE) ** (-2.0 * np.arange(half) / HD)
    steps = np.concatenate([np.arange(Layer.QB), np.arange(T // Layer.QB) * Layer.QB])
    angles = steps[:, None] * inv_freq[None, :]
    rc = jnp.asarray(np.cos(angles), jnp.float32)
    rs = jnp.asarray(np.sin(angles), jnp.float32)
    hbm, vmem = pl.BlockSpec(memory_space=HBM), pl.BlockSpec(memory_space=pltpu.VMEM)
    flops = 2 * T * E * d["COLS"] + 2 * T * T * HD * d["H"]
    return pl.pallas_call(
        functools.partial(layer_kernel, d),
        out_shape=(jax.ShapeDtypeStruct(x.shape, jnp.bfloat16),
                   jax.ShapeDtypeStruct((1, T, HD), jnp.bfloat16), jax.ShapeDtypeStruct((1, T, HD), jnp.bfloat16)),
        in_specs=[hbm, pl.BlockSpec(memory_space=pltpu.SMEM), vmem, vmem, vmem, hbm],
        out_specs=(hbm, hbm, hbm),
        scratch_shapes=layer_scratch(d),
        compiler_params=pltpu.CompilerParams(vmem_limit_bytes=VMEM_LIMIT),
        cost_estimate=pl.CostEstimate(flops=flops, bytes_accessed=4 * T * E + 2 * E * d["COLS"], transcendentals=0),
        name="layer",
    )(x, prompt_len, ln_row, rc, rs, w)


def solution(mesh):
    batch_spec = P(("pod", "d"))

    def local_layer(x, prompt_len, ln_shard, w_in_shard, w_out_shard):
        d = dims(mesh, x, w_in_shard, w_out_shard)
        w, ln_row = gather(d, mesh, ln_shard, w_in_shard, w_out_shard.T)
        return layer(d, x, prompt_len, ln_row, w)

    return jax.shard_map(local_layer, mesh=mesh,
                         in_specs=(batch_spec, batch_spec, P("d"), P("d", None), P(None, "d")),
                         out_specs=(batch_spec, batch_spec, batch_spec), check_vma=False)
```

time: 693 us -> 657 us (0.948)
  Pallas kernels: 0 us -> 652 us
  matrix products: 403 us -> 0 us
  waiting for transfers between devices: 157 us -> 0 us
  blocking collectives: 50.5 us -> 0 us
  other arithmetic: 38.6 us -> 0 us
  local copies, waits for them, and re-layouts: 21.2 us -> 1.34 us
  between operations: 15.3 us -> 1.47 us
    pallas_call x0 -> x2, Pallas kernels: none -> 652 us  [the longest x1 328 us: gather(): pl.pallas_call(functools.partial(gather_kernel, d), out_shape=(jax.ShapeD...]
    dot_general x4 -> x0, matrix products: 350 us -> none  [the longest x1 185 us: layer_math(): jnp.einsum('bte,ec->btc', h_norm, w_in, preferred_element_type=jnp.float32)]
    all_gather x2 -> x0, waiting for transfers between devices: 156 us -> none  [the longest x1 156 us: local_layer(): w_in = lax.all_gather(w_in_shard, 'd', axis=0, tiled=True)]
    sub x1 -> x0, matrix products: 53 us -> none  [mix_tokens(): jax.nn.softmax(jnp.where(allowed, scores, -1e+30), axis=-1)]
    unnamed x1 -> x0, blocking collectives: 50.5 us -> none
    slice x4 -> x0, local copies, waits for them, and re-layouts: 14.2 us -> none  [the longest x1 6.41 us: apply_rope(): upper_half = rope_in[..., half_dim:]]
    concatenate x2 -> x0, other arithmetic: 13 us -> none  [apply_rope(): jnp.concatenate([lower_half * cos_b - upper_half * sin_b, upper_half * co...]
    reduce_sum x2 -> x0, other arithmetic: 10.2 us -> none  [the longest x1 5.69 us: layer_norm(): var_val = jnp.mean(centered * centered, axis=-1, keepdims=True)]
  transfers between devices with their start and end apart: 2 -> 0, of which waited for: 1 -> 0; matrix products, arithmetic and copies ran while one was open for 50% -> 0% of each run, Pallas kernels for 0% -> 0%
where the time goes in v1:
time: 657 us; the launch traced here: 655 us
  Pallas kernels  652 us (99%)
    pallas_call x1, Pallas kernels, gather(): pl.pallas_call(functools.partial(gather_kernel, d), out_shape=(jax.ShapeD...  328 us
    pallas_call x1, Pallas kernels, layer(): pl.pallas_call(functools.partial(layer_kernel, d), out_shape=(jax.ShapeDt...  325 us

profile of v1, /device:TPU:96, one launch (start us, length us, event | category | flops | bytes accessed | tf_op | source)
XLA Modules:
  0.0 655.2 jit_solution(5334127522001606021)
XLA Ops:
  1.3 0.7 tile.2
  1.9 0.1 broadcast_in_dim.7
  2.0 0.6 broadcast_in_dim.8.ln_ref
  2.6 327.7 %gather.1 = (bf16[4,4,2,64,29184]{4,3,2,1,0:T(8,128)(2,1)}, f32[1,2048]{1,0:T(1,128)}) custom-call(f32[8,128]{1,0:T(8,128)} %broadcast_in_dim.8.ln_ref, bf16[64,18944]{1,0:T(8,128)(2,1)} %win_ref.1, bf16[64,10240]{1,0:T(8,128)(2,1)} %bitcast.1), custom_call_target="tpu_custom_call" | custom-call | tf_op jit(solution)/shard_map/gather/pallas_call | solution.py:221
  330.3 324.7 %layer.1 = (bf16[1,2048,2048]{2,1,0:T(8,128)(2,1)}, bf16[1,2048,256]{2,1,0:T(8,128)(2,1)}, bf16[1,2048,256]{2,1,0:T(8,128)(2,1)}) custom-call(bf16[1,2048,2048]{2,1,0:T(8,128)(2,1)} %refs_0_.1, s32[1]{0:T(128)S(6)} %copy.10.refs_1_, f32[1,2048]{1,0:T(1,128)} %get-tuple-element.5.refs_2_, f32[264,128]{1,0:T(8,128)} %constant.4.clone.refs_3_, ...), custom_call_target="tpu_custom_call" | custom-call | flops 261993005056 | bytes 136314880 | tf_op jit(solution)/shard_map/layer/pallas_call | solution.py:507

commit v2 on v1

--- a/solution.py
+++ b/solution.py
@@ -16,8 +16,9 @@
 HBM = pltpu.HBM
 VMEM_LIMIT = 67043328
 
-CHUNK = 384
-LAG = (0, 2, 4, 6, 8, 10)
+CHUNK = 768
+LAG = (0, 1, 2, 4, 6, 7)
+HEAD_POINTS = 10
 
 
 def dims(mesh, x, w_in, w_out):
@@ -30,12 +31,6 @@
     head = (w_in.shape[1] - 2 * ffn - attn) // 2
     return dict(D=devices, CORES=cores, SIDE=side, T=x.shape[1], E=model, F=ffn, H=attn // head, HD=head,
                 R=model // devices, COLS=w_in.shape[1] + w_out.shape[0], FC=head)
-
-
-def rope_tables(seq_len, head_dim):
-    half = head_dim // 2
-    inv_freq = np.float32(ROPE_BASE) ** (np.float32(-2.0) * np.arange(half, dtype=np.float32) / np.float32(head_dim))
-    return inv_freq
 
 
 def place():
@@ -192,51 +187,6 @@
         row_ref[0:1, i * 128:(i + 1) * 128] = part
 
 
-def gather_kernel(d, ln_ref, win_ref, wot_ref, w_ref, lnout_ref, stage_ref, ln_all, local_sem, ln_send, ln_recv,
-                  send_sem, recv_sem):
-    order_copies(d, win_ref, wot_ref, stage_ref, local_sem.at[0])
-    comm = Comm(d, stage_ref, w_ref, send_sem, recv_sem)
-    own = pltpu.make_async_copy(stage_ref, w_ref.at[comm.y, comm.x, comm.core], local_sem.at[1])
-    meet(d)
-    spread_scale(d, ln_ref, ln_all, ln_send, ln_recv)
-    pltpu.make_async_copy(stage_ref, stage_ref, local_sem.at[0]).wait()
-    own.start()
-    spread_scale_wait(d, ln_all, ln_send, ln_recv)
-    comm.point(0)
-    comm.point(1)
-    own.wait()
-
-    @pl.loop(2, comm.groups + LAG[5])
-    def _(p):
-        comm.point(p)
-
-    comm.drain()
-    scale_row(d, ln_all, lnout_ref)
-
-
-def gather(d, mesh, ln, w_in, wot):
-    groups = d["COLS"] // CHUNK
-    ln_tile = jnp.broadcast_to(jnp.tile(ln, 128 // d["R"])[None], (8, 128))
-    w_shape = (d["SIDE"], d["SIDE"], d["CORES"], d["R"], d["COLS"])
-    return pl.pallas_call(
-        functools.partial(gather_kernel, d),
-        out_shape=(jax.ShapeDtypeStruct(w_shape, jnp.bfloat16), jax.ShapeDtypeStruct((1, d["E"]), jnp.float32)),
-        in_specs=[pl.BlockSpec(memory_space=pltpu.VMEM), pl.BlockSpec(memory_space=HBM), pl.BlockSpec(memory_space=HBM)],
-        out_specs=(pl.BlockSpec(memory_space=HBM), pl.BlockSpec(memory_space=pltpu.VMEM)),
-        scratch_shapes=[
-            pltpu.VMEM((d["R"], d["COLS"]), jnp.bfloat16),
-            pltpu.VMEM((d["D"], 8, 128), jnp.float32),
-            pltpu.SemaphoreType.DMA((2,)),
-            pltpu.SemaphoreType.DMA,
-            pltpu.SemaphoreType.DMA,
-            pltpu.SemaphoreType.DMA((5,)),
-            pltpu.SemaphoreType.DMA((5, groups)),
-        ],
-        compiler_params=pltpu.CompilerParams(collective_id=0, has_side_effects=True, vmem_limit_bytes=VMEM_LIMIT),
-        name="gather",
-    )(ln_tile, w_in, wot)
-
-
 def nn(a, b):
     return lax.dot_general(a, b, (((1,), (0,)), ((), ())), preferred_element_type=jnp.float32)
 
@@ -259,9 +209,13 @@
     def __init__(self, d, r):
         self.d, self.r = d, r
 
-    def x_copy(self, i, slot):
+    def x_copy(self, i):
         rows = pl.ds(pl.multiple_of(i * self.XB, self.XB), self.XB)
-        return pltpu.make_async_copy(self.r.x.at[0, rows, :], self.r.xbuf.at[slot], self.r.xsem.at[slot])
+        return pltpu.make_async_copy(self.r.x.at[0, rows, :], self.r.h.at[rows, :], self.r.xsem.at[i])
+
+    def y_copy(self, m):
+        rows = pl.ds(m * self.MB, self.MB)
+        return pltpu.make_async_copy(self.r.h.at[rows, :], self.r.y.at[0, rows, :], self.r.xsem.at[m])
 
     def unit(self, col, buf, sem):
         return pltpu.make_async_copy(self.r.w.at[:, :, :, :, pl.ds(pl.multiple_of(col, 128), self.d["FC"])], buf, sem)
@@ -269,26 +223,15 @@
     def wval(self, buf):
         return buf[...].reshape(self.d["E"], self.d["FC"])
 
-    def norm(self):
-        d, r = self.d, self.r
-        n = d["T"] // self.XB
-        self.x_copy(0, 0).start()
-
-        @pl.loop(0, n)
-        def _(i):
-            slot = lax.rem(i, 2)
-
-            @pl.when(i + 1 < n)
-            def _():
-                self.x_copy(i + 1, 1 - slot).start()
-
-            self.x_copy(i, slot).wait()
-            rows = pl.ds(pl.multiple_of(i * self.XB, self.XB), self.XB)
-            xf = r.xbuf[slot].astype(jnp.float32)
-            centered = xf - jnp.mean(xf, axis=-1, keepdims=True)
-            var = jnp.mean(centered * centered, axis=-1, keepdims=True)
-            r.h[rows, :] = (centered * lax.rsqrt(var + EPS) * r.ln[...]).astype(jnp.bfloat16)
-            r.yacc[rows, :] = xf
+    def norm(self, i):
+        r = self.r
+        self.x_copy(i).wait()
+        rows = pl.ds(pl.multiple_of(i * self.XB, self.XB), self.XB)
+        xf = r.h[rows, :].astype(jnp.float32)
+        centered = xf - jnp.mean(xf, axis=-1, keepdims=True)
+        var = jnp.mean(centered * centered, axis=-1, keepdims=True)
+        r.h[rows, :] = (centered * lax.rsqrt(var + EPS) * r.ln[...]).astype(jnp.bfloat16)
+        r.yacc[rows, :] = xf
 
     def tables(self):
         d, r = self.d, self.r
@@ -353,71 +296,65 @@
         hg = g * 0.5
         a_ref[rows, :] = ((hg + hg * jnp.tanh(hg)) * u).astype(jnp.bfloat16)
 
-    def finish(self):
+    def finish(self, a_ref, obuf):
         d, r = self.d, self.r
-        n = d["T"] // self.XB
-
-        def out(i, slot):
-            rows = pl.ds(pl.multiple_of(i * self.XB, self.XB), self.XB)
-            return pltpu.make_async_copy(r.xbuf.at[slot], r.y.at[0, rows, :], r.xsem.at[slot])
-
-        @pl.loop(0, n)
-        def _(i):
-            slot = lax.rem(i, 2)
-
-            @pl.when(i >= 2)
-            def _():
-                out(i - 2, slot).wait()
-
-            rows = pl.ds(pl.multiple_of(i * self.XB, self.XB), self.XB)
-            r.xbuf[slot] = r.yacc[rows, :].astype(jnp.bfloat16)
-            out(i, slot).start()
-
-        out(n - 2, n % 2).wait()
-        out(n - 1, 1 - n % 2).wait()
+        fc = d["FC"]
+        for m in range(d["T"] // self.MB):
+            rows = slice(m * self.MB, (m + 1) * self.MB)
+            for t in range(d["E"] // fc):
+                cols = slice(t * fc, (t + 1) * fc)
+                total = r.yacc[rows, cols] + nt(a_ref[rows, :], self.wval(obuf)[cols, :])
+                r.h[rows, cols] = total.astype(jnp.bfloat16)
+            self.y_copy(m).start()
+        for m in range(d["T"] // self.MB):
+            self.y_copy(m).wait()
 
 
 class Refs:
     pass
 
 
-LAYER_NAMES = ("x", "plen", "ln", "rc", "rs", "w", "y", "kc", "vc", "h", "yacc", "xbuf", "cos", "sin", "bias", "k", "v", "q", "o", "a",
-               "wbuf", "obuf", "xsem", "wsem", "osem", "csem")
-
-
-def layer_scratch(d):
+NAMES = ("ln_tile", "win", "wot", "x", "plen", "rc", "rs",
+         "y", "kc", "vc", "w",
+         "stage", "ln_all", "ln", "h", "yacc", "cos", "sin", "bias", "k", "v", "q", "o", "a", "wbuf", "obuf",
+         "local_sem", "ln_send", "ln_recv", "send_sem", "recv_sem", "xsem", "wsem", "osem", "csem")
+
+
+def scratch(d):
     T, E, HD, FC = d["T"], d["E"], d["HD"], d["FC"]
     unit = (d["SIDE"], d["SIDE"], d["CORES"], d["R"], FC)
+    bf16, f32, dma = jnp.bfloat16, jnp.float32, pltpu.SemaphoreType.DMA
     return [
-        pltpu.VMEM((T, E), jnp.bfloat16),
-        pltpu.VMEM((T, E), jnp.float32),
-        pltpu.VMEM((2, Layer.XB, E), jnp.bfloat16),
-        pltpu.VMEM((T, HD // 2), jnp.float32),
-        pltpu.VMEM((T, HD // 2), jnp.float32),
-        pltpu.VMEM((8, T), jnp.float32),
-        pltpu.VMEM((T, HD), jnp.bfloat16),
-        pltpu.VMEM((T, HD), jnp.bfloat16),
-        pltpu.VMEM((T, HD), jnp.bfloat16),
-        pltpu.VMEM((T, HD), jnp.bfloat16),
-        pltpu.VMEM((2, T, FC), jnp.bfloat16),
-        pltpu.VMEM((2, 2) + unit, jnp.bfloat16),
-        pltpu.VMEM((3,) + unit, jnp.bfloat16),
-        pltpu.SemaphoreType.DMA((2,)),
-        pltpu.SemaphoreType.DMA((2, 2)),
-        pltpu.SemaphoreType.DMA((3,)),
-        pltpu.SemaphoreType.DMA((2,)),
+        pltpu.VMEM((d["R"], d["COLS"]), bf16),
+        pltpu.VMEM((d["D"], 8, 128), f32),
+        pltpu.VMEM((1, E), f32),
+        pltpu.VMEM((T, E), bf16),
+        pltpu.VMEM((T, E), f32),
+        pltpu.VMEM((T, HD // 2), f32),
+        pltpu.VMEM((T, HD // 2), f32),
+        pltpu.VMEM((8, T), f32),
+        pltpu.VMEM((T, HD), bf16),
+        pltpu.VMEM((T, HD), bf16),
+        pltpu.VMEM((T, HD), bf16),
+        pltpu.VMEM((T, HD), bf16),
+        pltpu.VMEM((2, T, FC), bf16),
+        pltpu.VMEM((2, 2) + unit, bf16),
+        pltpu.VMEM((3,) + unit, bf16),
+        dma((2,)), dma, dma, dma((5,)), dma((5, d["COLS"] // CHUNK)),
+        dma((T // Layer.XB,)), dma((2, 2)), dma((3,)), dma((2,)),
     ]
 
 
-def layer_kernel(d, *refs):
+def kernel(d, *refs):
     r = Refs()
-    for name, ref in zip(LAYER_NAMES, refs, strict=True):
+    for name, ref in zip(NAMES, refs, strict=True):
         setattr(r, name, ref)
     L = Layer(d, r)
     HD, FC, H = d["HD"], d["FC"], d["H"]
     J = d["F"] // FC
     tiles = d["E"] // FC
     mbs = d["T"] // L.MB
+    xbs = d["T"] // L.XB
     base = 2 * HD + H * 2 * HD
 
     def fetch_kv():
@@ -425,13 +362,13 @@
 
     def fetch_head(h):
         col = 2 * HD + h * 2 * HD
-        return [L.unit(col, r.wbuf.at[1, lax.rem(h, 2)], r.wsem.at[1, lax.rem(h, 2)]),
-                L.unit(col + HD, r.obuf.at[lax.rem(h, 2)], r.osem.at[lax.rem(h, 2)])]
+        s = lax.rem(h, 2)
+        return [L.unit(col, r.wbuf.at[1, s], r.wsem.at[1, s]), L.unit(col + HD, r.obuf.at[s], r.osem.at[s])]
 
     def fetch_mlp(j):
         col = base + j * 3 * FC
         s = lax.rem(j, 2)
-        o = lax.rem(j, 3)
+        o = lax.rem(j + H, 3)
         return [L.unit(col, r.wbuf.at[s, 0], r.wsem.at[s, 0]), L.unit(col + FC, r.wbuf.at[s, 1], r.wsem.at[s, 1]),
                 L.unit(col + 2 * FC, r.obuf.at[o], r.osem.at[o])]
 
@@ -443,11 +380,62 @@
         for c in copies:
             c.wait()
 
-    start(fetch_kv())
-    start(fetch_head(0))
-    L.norm()
+    groups = d["COLS"] // CHUNK
+    total = groups + LAG[5]
+    first = LAG[5] + 2
+    over_mlp = max(total - first - HEAD_POINTS, 0)
+
+    def head_points(h):
+        return h * HEAD_POINTS // H
+
+    def mlp_points(j):
+        return j * over_mlp // (J - 1)
+
+    def ready(points):
+        return (points - LAG[5]) * CHUNK
+
+    assert ready(first) >= 2 * HD + 2 * HD
+    for h in range(H):
+        assert ready(first + head_points(h + 1)) >= min(2 * HD + (h + 2) * 2 * HD, base)
+    assert ready(first + HEAD_POINTS) >= base + 3 * FC
+    for j in range(J - 1):
+        assert ready(first + HEAD_POINTS + mlp_points(j + 1)) >= base + (j + 2) * 3 * FC, j
+
+    order_copies(d, r.win, r.wot, r.stage, r.local_sem.at[0])
+    for i in range(xbs):
+        L.x_copy(i).start()
+    comm = Comm(d, r.stage, r.w, r.send_sem, r.recv_sem)
+    own = pltpu.make_async_copy(r.stage, r.w.at[comm.y, comm.x, comm.core], r.local_sem.at[1])
+    meet(d)
+    spread_scale(d, r.ln_tile, r.ln_all, r.ln_send, r.ln_recv)
+    pltpu.make_async_copy(r.stage, r.stage, r.local_sem.at[0]).wait()
+    own.start()
+    for p in range(LAG[2]):
+        comm.point(p)
+    own.wait()
     L.tables()
     L.bias()
+    spread_scale_wait(d, r.ln_all, r.ln_send, r.ln_recv)
+    scale_row(d, r.ln_all, r.ln)
+    per = -(-xbs // (first - 1 - LAG[2]))
+
+    @pl.loop(LAG[2], first)
+    def _(p):
+        comm.point(p)
+
+        @pl.loop(0, per)
+        def _(k):
+            i = (p - LAG[2]) * per + k
+
+            @pl.when(i < xbs)
+            def _():
+                L.norm(i)
+
+        @pl.when(p == first - 2)
+        def _():
+            start(fetch_kv())
+
+    start(fetch_head(0))
     wait(fetch_kv())
     L.keys(r.wbuf.at[0, 0], r.wbuf.at[0, 1])
     pltpu.make_async_copy(r.k, r.kc.at[0], r.csem.at[0]).start()
@@ -455,9 +443,19 @@
 
     @pl.loop(0, H)
     def _(h):
+        lo, hi = lax.div(h * HEAD_POINTS, H), lax.div((h + 1) * HEAD_POINTS, H)
+
+        @pl.loop(first + lo, first + hi)
+        def _(p):
+            comm.point(p)
+
         @pl.when(h + 1 < H)
         def _():
             start(fetch_head(h + 1))
+
+        @pl.when(h + 1 == H)
+        def _():
+            start(fetch_mlp(0))
 
         wait(fetch_head(h))
         L.query(r.wbuf.at[1, lax.rem(h, 2)])
@@ -465,10 +463,17 @@
         for t in range(tiles):
             L.add_out(r.o, r.obuf.at[lax.rem(h, 2)], t)
 
-    start(fetch_mlp(0))
+    wait(fetch_mlp(0))
+
+    def mlp_point(j):
+        lo, hi = lax.div(j * over_mlp, J - 1), lax.div((j + 1) * over_mlp, J - 1)
+
+        @pl.loop(first + HEAD_POINTS + lo, first + HEAD_POINTS + hi)
+        def _(p):
+            comm.point(p)
+
+    mlp_point(0)
     start(fetch_mlp(1))
-
-    wait(fetch_mlp(0))
     for m in range(mbs):
         L.gated(m, r.wbuf.at[0, 0], r.wbuf.at[0, 1], r.a.at[0])
 
@@ -476,25 +481,25 @@
     def _(j):
         @pl.when(j + 1 < J)
         def _():
+            mlp_point(j)
             start(fetch_mlp(j + 1))
 
         wait(fetch_mlp(j))
         s = lax.rem(j, 2)
-        prev = r.obuf.at[lax.rem(j - 1, 3)]
+        prev = r.obuf.at[lax.rem(j - 1 + H, 3)]
         per = tiles // mbs
         for m in range(mbs):
             L.gated(m, r.wbuf.at[s, 0], r.wbuf.at[s, 1], r.a.at[s])
             for t in range(m * per, (m + 1) * per):
                 L.add_out(r.a.at[1 - s], prev, t)
 
-    for t in range(tiles):
-        L.add_out(r.a.at[(J - 1) % 2], r.obuf.at[(J - 1) % 3], t)
-    L.finish()
+    L.finish(r.a.at[(J - 1) % 2], r.obuf.at[(J - 1 + H) % 3])
     pltpu.make_async_copy(r.k, r.kc.at[0], r.csem.at[0]).wait()
     pltpu.make_async_copy(r.v, r.vc.at[0], r.csem.at[1]).wait()
-
-
-def layer(d, x, prompt_len, ln_row, w):
+    comm.drain()
+
+
+def layer(d, x, prompt_len, ln, w_in, wot):
     T, E, HD = d["T"], d["E"], d["HD"]
     half = HD // 2
     inv_freq = np.float64(ROPE_BASE) ** (-2.0 * np.arange(half) / HD)
@@ -502,19 +507,23 @@
     angles = steps[:, None] * inv_freq[None, :]
     rc = jnp.asarray(np.cos(angles), jnp.float32)
     rs = jnp.asarray(np.sin(angles), jnp.float32)
+    ln_tile = jnp.broadcast_to(jnp.tile(ln, 128 // d["R"])[None], (8, 128))
+    w_shape = (d["SIDE"], d["SIDE"], d["CORES"], d["R"], d["COLS"])
     hbm, vmem = pl.BlockSpec(memory_space=HBM), pl.BlockSpec(memory_space=pltpu.VMEM)
     flops = 2 * T * E * d["COLS"] + 2 * T * T * HD * d["H"]
-    return pl.pallas_call(
-        functools.partial(layer_kernel, d),
-        out_shape=(jax.ShapeDtypeStruct(x.shape, jnp.bfloat16),
-                   jax.ShapeDtypeStruct((1, T, HD), jnp.bfloat16), jax.ShapeDtypeStruct((1, T, HD), jnp.bfloat16)),
-        in_specs=[hbm, pl.BlockSpec(memory_space=pltpu.SMEM), vmem, vmem, vmem, hbm],
-        out_specs=(hbm, hbm, hbm),
-        scratch_shapes=layer_scratch(d),
-        compiler_params=pltpu.CompilerParams(vmem_limit_bytes=VMEM_LIMIT),
+    cache = jax.ShapeDtypeStruct((1, T, HD), jnp.bfloat16)
+    y, kc, vc, _ = pl.pallas_call(
+        functools.partial(kernel, d),
+        out_shape=(jax.ShapeDtypeStruct(x.shape, jnp.bfloat16), cache, cache,
+                   jax.ShapeDtypeStruct(w_shape, jnp.bfloat16)),
+        in_specs=[vmem, hbm, hbm, hbm, pl.BlockSpec(memory_space=pltpu.SMEM), vmem, vmem],
+        out_specs=(hbm, hbm, hbm, hbm),
+        scratch_shapes=scratch(d),
+        compiler_params=pltpu.CompilerParams(collective_id=0, has_side_effects=True, vmem_limit_bytes=VMEM_LIMIT),
         cost_estimate=pl.CostEstimate(flops=flops, bytes_accessed=4 * T * E + 2 * E * d["COLS"], transcendentals=0),
         name="layer",
-    )(x, prompt_len, ln_row, rc, rs, w)
+    )(ln_tile, w_in, wot, x, prompt_len, rc, rs)
+    return y, kc, vc
 
 
 def solution(mesh):
@@ -522,8 +531,7 @@
 
     def local_layer(x, prompt_len, ln_shard, w_in_shard, w_out_shard):
         d = dims(mesh, x, w_in_shard, w_out_shard)
-        w, ln_row = gather(d, mesh, ln_shard, w_in_shard, w_out_shard.T)
-        return layer(d, x, prompt_len, ln_row, w)
+        return layer(d, x, prompt_len, ln_shard, w_in_shard, w_out_shard.T)
 
     return jax.shard_map(local_layer, mesh=mesh,
                          in_specs=(batch_spec, batch_spec, P("d"), P("d", None), P(None, "d")),

time: 657 us -> 407 us (0.62)
  Pallas kernels: 652 us -> 393 us
  local copies, waits for them, and re-layouts: 1.34 us -> 11.9 us
    pallas_call x2 -> x1, Pallas kernels: 652 us -> 393 us  [layer(): pl.pallas_call(functools.partial(kernel, d), out_shape=(jax.ShapeDtypeStr...]
    unnamed x0 -> x7, local copies, waits for them, and re-layouts: none -> 10.5 us
where the time goes in v2:
time: 407 us; the launch traced here: 406 us
  Pallas kernels  393 us (97%)
  local copies, waits for them, and re-layouts  11.9 us (3%)
    pallas_call x1, Pallas kernels, layer(): pl.pallas_call(functools.partial(kernel, d), out_shape=(jax.ShapeDtypeStr...  393 us
    unnamed x7, local copies, waits for them, and re-layouts  10.5 us

profile of v2, /device:TPU:96, one launch (start us, length us, event | category | flops | bytes accessed | tf_op | source)
XLA Modules:
  0.0 406.4 jit_solution(294547668387081077)
XLA Ops:
  1.3 0.7 tile.2
  1.9 0.1 broadcast_in_dim.7
  2.0 0.6 broadcast_in_dim.8.refs_0_
  2.6 393.3 %layer.1 = (bf16[1,2048,2048]{2,1,0:T(8,128)(2,1)}, bf16[1,2048,256]{2,1,0:T(8,128)(2,1)}, bf16[1,2048,256]{2,1,0:T(8,128)(2,1)}, bf16[4,4,2,64,29184]{4,3,2,1,0:T(8,128)(2,1)}) custom-call(f32[8,128]{1,0:T(8,128)} %broadcast_in_dim.8.refs_0_, bf16[64,18944]{1,0:T(8,128)(2,1)} %refs_1_.1, bf16[64,10240]{1,0:T(8,128)(2,1)} %bitcast.1, ...), custom_call_target="tpu_custom_call" | custom-call | flops 261993005056 | bytes 136314880 | tf_op jit(solution)/shard_map/layer/pallas_call | solution.py:515
  395.9 0.0 copy-start.1
  395.9 0.0 copy-start
  395.9 8.6 %copy.14 = bf16[1,2048,2048]{2,1,0:T(8,128)(2,1)} copy(bf16[1,2048,2048]{2,1,0:T(8,128)(2,1)} %get-tuple-element.12) | data formatting | bytes 16777216
  404.5 0.0 copy-done.1
  404.5 1.0 copy.15
  405.5 0.0 copy-done
  405.5 1.0 copy.16
Async XLA Ops:
  395.9 8.6 %copy-start.1 = (bf16[1,2048,256]{2,1,0:T(8,128)(2,1)S(1)}, bf16[1,2048,256]{2,1,0:T(8,128)(2,1)}, u32[]{:S(2)}) copy-start(bf16[1,2048,256]{2,1,0:T(8,128)(2,1)} %get-tuple-element.13) | copy-start | bytes 3145732
  395.9 9.6 %copy-start = (bf16[1,2048,256]{2,1,0:T(8,128)(2,1)S(1)}, bf16[1,2048,256]{2,1,0:T(8,128)(2,1)}, u32[]{:S(2)}) copy-start(bf16[1,2048,256]{2,1,0:T(8,128)(2,1)} %get-tuple-element.14) | copy-start | bytes 3145732

commit v3 on v2

--- a/solution.py
+++ b/solution.py
@@ -17,8 +17,8 @@
 VMEM_LIMIT = 67043328
 
 CHUNK = 768
-LAG = (0, 1, 2, 4, 6, 7)
-HEAD_POINTS = 10
+LAG = (0, 2, 4, 6, 8, 9)
+HEAD_POINTS = 8
 
 
 def dims(mesh, x, w_in, w_out):
@@ -132,7 +132,7 @@
             self.landed(w.at[:, :, 0, :, cols], 4, g)
 
     def point(self, p):
-        for stage in range(6):
+        for stage in (4, 3, 2, 1, 0, 5):
             g = p - LAG[stage]
             if isinstance(g, int):
                 if 0 <= g < self.groups:
@@ -253,31 +253,80 @@
         for m in range(d["T"] // self.MB):
             rows = slice(m * self.MB, (m + 1) * self.MB)
             hb = r.h[rows, :]
-            r.k[rows, :] = rope(nn(hb, self.wval(kbuf)), r.cos[rows, :], r.sin[rows, :]).astype(jnp.bfloat16)
+            kf = rope(nn(hb, self.wval(kbuf)), r.cos[rows, :], r.sin[rows, :])
+            r.k[rows, :] = kf.astype(jnp.bfloat16)
+            r.kt[:, rows] = kf.T.astype(jnp.bfloat16)
             r.v[rows, :] = nn(hb, self.wval(vbuf)).astype(jnp.bfloat16)
 
-    def query(self, qbuf):
-        r, d = self.r, self.d
-        scale = 1.0 / math.sqrt(d["HD"])
-        for m in range(d["T"] // self.MB):
-            rows = slice(m * self.MB, (m + 1) * self.MB)
-            q = rope(nn(r.h[rows, :], self.wval(qbuf)), r.cos[rows, :], r.sin[rows, :]).astype(jnp.bfloat16)
-            r.q[rows, :] = q * jnp.bfloat16(scale)
-
-    def attend(self):
-        r, d = self.r, self.d
-        qb = self.QB
-        row = lax.broadcasted_iota(jnp.int32, (qb, qb), 0)
-        col = lax.broadcasted_iota(jnp.int32, (qb, qb), 1)
-        for b in range(d["T"] // qb):
-            n = (b + 1) * qb
-            rows = slice(b * qb, n)
-            s = nt(r.q[rows, :], r.k[0:n, :]) + r.bias[0:1, 0:n]
-            last = jnp.where(col <= row, s[:, n - qb:], MASKED)
-            s = last if b == 0 else jnp.concatenate([s[:, :n - qb], last], axis=1)
-            e = jnp.exp(s - jnp.max(s, axis=-1, keepdims=True))
-            p = (e * (1.0 / jnp.sum(e, axis=-1, keepdims=True))).astype(jnp.bfloat16)
-            r.o[rows, :] = nn(p, r.v[0:n, :]).astype(jnp.bfloat16)
+    def query(self, m, qbuf, q_ref):
+        r = self.r
+        rows = slice(m * self.MB, (m + 1) * self.MB)
+        q_ref[rows, :] = rope(nn(r.h[rows, :], self.wval(qbuf)), r.cos[rows, :], r.sin[rows, :]).astype(jnp.bfloat16)
+
+    def scores(self, b, q_ref, z_ref):
+        d, r = self.d, self.r
+        qb, half = self.QB, self.QB // 2
+        unit = math.log2(math.e) / math.sqrt(d["HD"])
+        q = q_ref[b * qb:(b + 1) * qb, :]
+        top = [None, None]
+        for c in range(b + 1):
+            cols = slice(c * qb, (c + 1) * qb)
+            s = nn(q, r.kt[:, cols])
+            for i in range(2):
+                part = slice(i * half, (i + 1) * half)
+                z = s[part, :] * unit + r.bias[0:1, cols]
+                if c == b:
+                    row = lax.broadcasted_iota(jnp.int32, (half, qb), 0) + i * half
+                    col = lax.broadcasted_iota(jnp.int32, (half, qb), 1)
+                    z = jnp.where(col <= row, z, MASKED)
+                z_ref[part, cols] = z
+                for k in range(qb // 128):
+                    zk = z[:, k * 128:(k + 1) * 128]
+                    top[i] = zk if top[i] is None else jnp.maximum(top[i], zk)
+        return [jnp.max(t, axis=-1, keepdims=True) for t in top]
+
+    def softmax(self, b, z_ref, p_ref, top):
+        qb, half = self.QB, self.QB // 2
+        for i in range(2):
+            part = slice(i * half, (i + 1) * half)
+            total = None
+            for c in range(b + 1):
+                cols = slice(c * qb, (c + 1) * qb)
+                e = jnp.exp2(z_ref[part, cols] - top[i])
+                z_ref[part, cols] = e
+                for k in range(qb // 128):
+                    ek = e[:, k * 128:(k + 1) * 128]
+                    total = ek if total is None else total + ek
+            inv = 1.0 / jnp.sum(total, axis=-1, keepdims=True)
+            for c in range(b + 1):
+                cols = slice(c * qb, (c + 1) * qb)
+                p_ref[part, cols] = (z_ref[part, cols] * inv).astype(jnp.bfloat16)
+
+    def values(self, b, p_ref, o_ref):
+        r, qb = self.r, self.QB
+        n = (b + 1) * qb
+        o_ref[b * qb:n, :] = nn(p_ref[:, 0:n], r.v[0:n, :]).astype(jnp.bfloat16)
+
+    def head(self, q_ref, o_ref, q_next, qbuf_next, o_prev, obuf_prev):
+        d, r = self.d, self.r
+        nb = d["T"] // self.QB
+        mbs, tiles = d["T"] // self.MB, d["E"] // d["FC"]
+        work = [functools.partial(self.add_out, o_prev, obuf_prev, t) for t in range(tiles)]
+        per = tiles // mbs
+        steps = []
+        for m in range(mbs):
+            steps += [work[m * per:(m + 1) * per], [functools.partial(self.query, m, qbuf_next, q_next)]]
+        last = None
+        for n, b in enumerate(reversed(range(nb))):
+            z_ref, p_ref = r.z.at[n % 2], r.p.at[n % 2]
+            top = self.scores(b, q_ref, z_ref)
+            for f in steps[n]:
+                f()
+            self.softmax(b, z_ref, p_ref, top)
+            if last is not None:
+                self.values(*last)
+            last = (b, p_ref, o_ref)
+        self.values(*last)
 
     def add_out(self, a_ref, obuf, tile):
         r, d = self.r, self.d
@@ -316,7 +365,7 @@
 
 NAMES = ("ln_tile", "win", "wot", "x", "plen", "rc", "rs",
          "y", "kc", "vc", "w",
-         "stage", "ln_all", "ln", "h", "yacc", "cos", "sin", "bias", "k", "v", "q", "o", "a", "wbuf", "obuf",
+         "stage", "ln_all", "ln", "h", "yacc", "cos", "sin", "bias", "k", "kt", "v", "q", "o", "z", "p", "a", "wbuf", "obuf",
          "local_sem", "ln_send", "ln_recv", "send_sem", "recv_sem", "xsem", "wsem", "osem", "csem")
 
 
@@ -334,9 +383,12 @@
         pltpu.VMEM((T, HD // 2), f32),
         pltpu.VMEM((8, T), f32),
         pltpu.VMEM((T, HD), bf16),
+        pltpu.VMEM((HD, T), bf16),
         pltpu.VMEM((T, HD), bf16),
-        pltpu.VMEM((T, HD), bf16),
-        pltpu.VMEM((T, HD), bf16),
+        pltpu.VMEM((2, T, HD), bf16),
+        pltpu.VMEM((2, T, HD), bf16),
+        pltpu.VMEM((2, Layer.QB, T), f32),
+        pltpu.VMEM((2, Layer.QB, T), bf16),
         pltpu.VMEM((2, T, FC), bf16),
         pltpu.VMEM((2, 2) + unit, bf16),
         pltpu.VMEM((3,) + unit, bf16),
@@ -360,10 +412,13 @@
     def fetch_kv():
         return [L.unit(0, r.wbuf.at[0, 0], r.wsem.at[0, 0]), L.unit(HD, r.wbuf.at[0, 1], r.wsem.at[0, 1])]
 
-    def fetch_head(h):
-        col = 2 * HD + h * 2 * HD
+    def fetch_q(h):
         s = lax.rem(h, 2)
-        return [L.unit(col, r.wbuf.at[1, s], r.wsem.at[1, s]), L.unit(col + HD, r.obuf.at[s], r.osem.at[s])]
+        return [L.unit(2 * HD + h * 2 * HD, r.wbuf.at[1, s], r.wsem.at[1, s])]
+
+    def fetch_o(h):
+        s = lax.rem(h, 3)
+        return [L.unit(2 * HD + h * 2 * HD + HD, r.obuf.at[s], r.osem.at[s])]
 
     def fetch_mlp(j):
         col = base + j * 3 * FC
@@ -395,8 +450,9 @@
         return (points - LAG[5]) * CHUNK
 
     assert ready(first) >= 2 * HD + 2 * HD
+    assert ready(first) >= 2 * HD + 3 * HD
     for h in range(H):
-        assert ready(first + head_points(h + 1)) >= min(2 * HD + (h + 2) * 2 * HD, base)
+        assert ready(first + head_points(h + 1)) >= min(2 * HD + (h + 2) * 2 * HD + HD, base)
     assert ready(first + HEAD_POINTS) >= base + 3 * FC
     for j in range(J - 1):
         assert ready(first + HEAD_POINTS + mlp_points(j + 1)) >= base + (j + 2) * 3 * FC, j
@@ -421,7 +477,8 @@
 
     @pl.loop(LAG[2], first)
     def _(p):
-        comm.point(p)
+        with jax.named_scope("point_start"):
+            comm.point(p)
 
         @pl.loop(0, per)
         def _(k):
@@ -435,11 +492,19 @@
         def _():
             start(fetch_kv())
 
-    start(fetch_head(0))
-    wait(fetch_kv())
+    start(fetch_q(0))
+    with jax.named_scope("wait_kv"):
+        wait(fetch_kv())
     L.keys(r.wbuf.at[0, 0], r.wbuf.at[0, 1])
     pltpu.make_async_copy(r.k, r.kc.at[0], r.csem.at[0]).start()
     pltpu.make_async_copy(r.v, r.vc.at[0], r.csem.at[1]).start()
+    start(fetch_q(1))
+    start(fetch_o(0))
+    wait(fetch_q(0))
+    for m in range(mbs):
+        L.query(m, r.wbuf.at[1, 0], r.q.at[0])
+    r.o[1] = jnp.zeros((d["T"], HD), jnp.bfloat16)
+    r.obuf[2] = jnp.zeros(r.obuf.shape[1:], jnp.bfloat16)
 
     @pl.loop(0, H)
     def _(h):
@@ -447,22 +512,31 @@
 
         @pl.loop(first + lo, first + hi)
         def _(p):
-            comm.point(p)
+            with jax.named_scope("point_head"):
+                comm.point(p)
 
         @pl.when(h + 1 < H)
         def _():
-            start(fetch_head(h + 1))
+            wait(fetch_q(h + 1))
+            start(fetch_o(h + 1))
+
+        @pl.when(h + 2 < H)
+        def _():
+            start(fetch_q(h + 2))
+
+        @pl.when(h > 0)
+        def _():
+            wait(fetch_o(h - 1))
 
         @pl.when(h + 1 == H)
         def _():
             start(fetch_mlp(0))
 
-        wait(fetch_head(h))
-        L.query(r.wbuf.at[1, lax.rem(h, 2)])
-        L.attend()
-        for t in range(tiles):
-            L.add_out(r.o, r.obuf.at[lax.rem(h, 2)], t)
-
+        s = lax.rem(h, 2)
+        with jax.named_scope("head"):
+            L.head(r.q.at[s], r.o.at[s], r.q.at[1 - s], r.wbuf.at[1, 1 - s], r.o.at[1 - s], r.obuf.at[lax.rem(h + 2, 3)])
+
+    wait(fetch_o(H - 1))
     wait(fetch_mlp(0))
 
     def mlp_point(j):
@@ -470,12 +544,16 @@
 
         @pl.loop(first + HEAD_POINTS + lo, first + HEAD_POINTS + hi)
         def _(p):
-            comm.point(p)
+            with jax.named_scope("point_mlp"):
+                comm.point(p)
 
     mlp_point(0)
     start(fetch_mlp(1))
+    per = tiles // mbs
     for m in range(mbs):
         L.gated(m, r.wbuf.at[0, 0], r.wbuf.at[0, 1], r.a.at[0])
+        for t in range(m * per, (m + 1) * per):
+            L.add_out(r.o.at[(H - 1) % 2], r.obuf.at[(H - 1) % 3], t)
 
     @pl.loop(1, J)
     def _(j):
@@ -484,16 +562,19 @@
             mlp_point(j)
             start(fetch_mlp(j + 1))
 
-        wait(fetch_mlp(j))
+        with jax.named_scope("wait_mlp"):
+            wait(fetch_mlp(j))
         s = lax.rem(j, 2)
         prev = r.obuf.at[lax.rem(j - 1 + H, 3)]
         per = tiles // mbs
-        for m in range(mbs):
-            L.gated(m, r.wbuf.at[s, 0], r.wbuf.at[s, 1], r.a.at[s])
-            for t in range(m * per, (m + 1) * per):
-                L.add_out(r.a.at[1 - s], prev, t)
-
-    L.finish(r.a.at[(J - 1) % 2], r.obuf.at[(J - 1 + H) % 3])
+        with jax.named_scope("mlp"):
+            for m in range(mbs):
+                L.gated(m, r.wbuf.at[s, 0], r.wbuf.at[s, 1], r.a.at[s])
+                for t in range(m * per, (m + 1) * per):
+                    L.add_out(r.a.at[1 - s], prev, t)
+
+    with jax.named_scope("finish"):
+        L.finish(r.a.at[(J - 1) % 2], r.obuf.at[(J - 1 + H) % 3])
     pltpu.make_async_copy(r.k, r.kc.at[0], r.csem.at[0]).wait()
     pltpu.make_async_copy(r.v, r.vc.at[0], r.csem.at[1]).wait()
     comm.drain()

time: 407 us -> 388 us (0.953)
  Pallas kernels: 393 us -> 375 us
    pallas_call x1, Pallas kernels: 393 us -> 375 us  [layer(): pl.pallas_call(functools.partial(kernel, d), out_shape=(jax.ShapeDtypeStr...]
where the time goes in v3:
time: 388 us
  Pallas kernels  375 us (97%)
  local copies, waits for them, and re-layouts  11.9 us (3%)
    pallas_call x1, Pallas kernels, layer(): pl.pallas_call(functools.partial(kernel, d), out_shape=(jax.ShapeDtypeStr...  375 us
    unnamed x7, local copies, waits for them, and re-layouts  10.5 us

profile of v3, /device:TPU:96, one launch (start us, length us, event | category | flops | bytes accessed | tf_op | source)
XLA Modules:
  0.0 387.9 jit_solution(3273944392763065411)
XLA Ops:
  1.3 0.7 tile.2
  1.9 0.1 broadcast_in_dim.7
  2.0 0.6 broadcast_in_dim.8.refs_0_
  2.6 374.7 %layer.1 = (bf16[1,2048,2048]{2,1,0:T(8,128)(2,1)}, bf16[1,2048,256]{2,1,0:T(8,128)(2,1)}, bf16[1,2048,256]{2,1,0:T(8,128)(2,1)}, bf16[4,4,2,64,29184]{4,3,2,1,0:T(8,128)(2,1)}) custom-call(f32[8,128]{1,0:T(8,128)} %broadcast_in_dim.8.refs_0_, bf16[64,18944]{1,0:T(8,128)(2,1)} %refs_1_.1, bf16[64,10240]{1,0:T(8,128)(2,1)} %bitcast.1, ...), custom_call_target="tpu_custom_call" | custom-call | flops 261993005056 | bytes 136314880 | tf_op jit(solution)/shard_map/layer/pallas_call | solution.py:596
  377.3 0.0 copy-start.1
  377.4 0.0 copy-start
  377.4 8.6 %copy.14 = bf16[1,2048,2048]{2,1,0:T(8,128)(2,1)} copy(bf16[1,2048,2048]{2,1,0:T(8,128)(2,1)} %get-tuple-element.12) | data formatting | bytes 16777216
  386.0 0.0 copy-done.1
  386.0 1.0 copy.15
  386.9 0.0 copy-done
  386.9 1.0 copy.16
Async XLA Ops:
  377.3 8.6 %copy-start.1 = (bf16[1,2048,256]{2,1,0:T(8,128)(2,1)S(1)}, bf16[1,2048,256]{2,1,0:T(8,128)(2,1)}, u32[]{:S(2)}) copy-start(bf16[1,2048,256]{2,1,0:T(8,128)(2,1)} %get-tuple-element.13) | copy-start | bytes 3145732
  377.4 9.6 %copy-start = (bf16[1,2048,256]{2,1,0:T(8,128)(2,1)S(1)}, bf16[1,2048,256]{2,1,0:T(8,128)(2,1)}, u32[]{:S(2)}) copy-start(bf16[1,2048,256]{2,1,0:T(8,128)(2,1)} %get-tuple-element.14) | copy-start | bytes 3145732

commit v4 on v3

--- a/solution.py
+++ b/solution.py
@@ -16,9 +16,16 @@
 HBM = pltpu.HBM
 VMEM_LIMIT = 67043328
 
-CHUNK = 768
+SMALL, SMALL_WIDTH, WIDTH = 20, 384, 768
 LAG = (0, 2, 4, 6, 8, 9)
-HEAD_POINTS = 8
+FIRST = 12
+NORM, KEYS, QUERY = 6, 7, 8
+OPENING = (
+    (0, 0), (0, 1), (0, 2), (0, 3), (0, 4), (0, 5), (0, 6), (1, 0), (1, 1), (0, 7), (1, 2), (1, 3), (0, 8), (1, 4),
+    (NORM, 2), (1, 5), (NORM, 1), (1, 6), (NORM, 1), (2, 0), (2, 1), (NORM, 11), (1, 7), (NORM, 1), (1, 8), (0, 9),
+    (3, 0), (2, 2), (3, 1), (2, 3), (4, 0), (1, 9), (0, 10), (3, 2), (2, 4), (4, 1), (5, 0), (3, 3), (2, 5), (5, 1),
+    (KEYS, 1), (4, 2), (KEYS, 1), (1, 10), (4, 3), (KEYS, 1), (3, 4), (2, 6), (KEYS, 1), (5, 2), (3, 5), (2, 7),
+    (QUERY, 2), (5, 3), (QUERY, 2), (0, 11))
 
 
 def dims(mesh, x, w_in, w_out):
@@ -68,14 +75,18 @@
     def __init__(self, d, stage_ref, w_ref, send_sem, recv_sem):
         self.d = d
         self.stage, self.w, self.send, self.recv = stage_ref, w_ref, send_sem, recv_sem
-        self.groups = d["COLS"] // CHUNK
+        self.groups = SMALL + (d["COLS"] - SMALL * SMALL_WIDTH) // WIDTH
+        self.done = [sum(1 for op in OPENING if op[0] == k) for k in range(6)]
         side, cores = d["SIDE"], d["CORES"]
         me = place()
-        self.me = me
         self.core = lax.rem(me, cores)
         self.x = lax.rem(lax.div(me, cores), side)
         self.y = lax.div(me, cores * side)
 
+    @staticmethod
+    def end(groups):
+        return min(groups, SMALL) * SMALL_WIDTH + max(groups - SMALL, 0) * WIDTH
+
     def dev(self, y, x, core):
         d = self.d
         return {"d": (y * d["SIDE"] + x) * d["CORES"] + core}
@@ -91,10 +102,13 @@
     def landed(self, ref, stage, g):
         pltpu.make_async_copy(ref, ref, self.recv.at[stage, g]).wait()
 
-    def stage_fn(self, stage, g):
+    def stage_fn(self, stage, g, small):
         w, x, y, c = self.w, self.x, self.y, self.core
         half = self.d["R"] // 2
-        cols = pl.ds(pl.multiple_of(g * CHUNK, 128), CHUNK)
+        if small:
+            cols = pl.ds(pl.multiple_of(g * SMALL_WIDTH, 128), SMALL_WIDTH)
+        else:
+            cols = pl.ds(pl.multiple_of(SMALL * SMALL_WIDTH + (g - SMALL) * WIDTH, 128), WIDTH)
         ra, rb = pl.ds(0, half), pl.ds(half, half)
         turn = 1 - 2 * lax.rem(g, 2)
         if stage == 0:
@@ -131,16 +145,17 @@
         else:
             self.landed(w.at[:, :, 0, :, cols], 4, g)
 
-    def point(self, p):
+    def point(self, p, lo, hi):
         for stage in (4, 3, 2, 1, 0, 5):
             g = p - LAG[stage]
-            if isinstance(g, int):
-                if 0 <= g < self.groups:
-                    self.stage_fn(stage, g)
-            else:
-                @pl.when(jnp.logical_and(g >= 0, g < self.groups))
-                def _(stage=stage, g=g):
-                    self.stage_fn(stage, g)
+            for small, start, stop in ((True, 0, SMALL), (False, SMALL, self.groups)):
+                start = max(start, self.done[stage])
+                if hi - 1 - LAG[stage] < start or lo - LAG[stage] >= stop:
+                    continue
+
+                @pl.when(jnp.logical_and(g >= start, g < stop))
+                def _(stage=stage, g=g, small=small):
+                    self.stage_fn(stage, g, small)
 
     def drain(self):
         side, w = self.d["SIDE"], self.w
@@ -149,7 +164,7 @@
             pltpu.make_async_copy(ref, ref, self.send.at[stage]).wait()
 
 
-def meet(d):
+def arrive(d):
     barrier = pltpu.get_barrier_semaphore()
     me = place()
 
@@ -157,7 +172,9 @@
     def _(i):
         pl.semaphore_signal(barrier, inc=1, device_id={"d": lax.rem(me + i, d["D"])}, device_id_type=MESH)
 
-    pl.semaphore_wait(barrier, d["D"] - 1)
+
+def meet(d):
+    pl.semaphore_wait(pltpu.get_barrier_semaphore(), d["D"] - 1)
 
 
 def spread_scale(d, ln_ref, ln_all, ln_send, ln_recv):
@@ -248,15 +265,14 @@
         col = lax.broadcasted_iota(jnp.int32, (8, d["T"]), 1)
         r.bias[...] = jnp.where(col < r.plen[0], 0.0, MASKED)
 
-    def keys(self, kbuf, vbuf):
-        r, d = self.r, self.d
-        for m in range(d["T"] // self.MB):
-            rows = slice(m * self.MB, (m + 1) * self.MB)
-            hb = r.h[rows, :]
-            kf = rope(nn(hb, self.wval(kbuf)), r.cos[rows, :], r.sin[rows, :])
-            r.k[rows, :] = kf.astype(jnp.bfloat16)
-            r.kt[:, rows] = kf.T.astype(jnp.bfloat16)
-            r.v[rows, :] = nn(hb, self.wval(vbuf)).astype(jnp.bfloat16)
+    def keys(self, m, kbuf, vbuf):
+        r = self.r
+        rows = slice(m * self.MB, (m + 1) * self.MB)
+        hb = r.h[rows, :]
+        kf = rope(nn(hb, self.wval(kbuf)), r.cos[rows, :], r.sin[rows, :])
+        r.k[rows, :] = kf.astype(jnp.bfloat16)
+        r.kt[:, rows] = kf.T.astype(jnp.bfloat16)
+        r.v[rows, :] = nn(hb, self.wval(vbuf)).astype(jnp.bfloat16)
 
     def query(self, m, qbuf, q_ref):
         r = self.r
@@ -307,7 +323,7 @@
         n = (b + 1) * qb
         o_ref[b * qb:n, :] = nn(p_ref[:, 0:n], r.v[0:n, :]).astype(jnp.bfloat16)
 
-    def head(self, q_ref, o_ref, q_next, qbuf_next, o_prev, obuf_prev):
+    def head(self, q_ref, o_ref, q_next, qbuf_next, o_prev, obuf_prev, midway):
         d, r = self.d, self.r
         nb = d["T"] // self.QB
         mbs, tiles = d["T"] // self.MB, d["E"] // d["FC"]
@@ -318,6 +334,8 @@
             steps += [work[m * per:(m + 1) * per], [functools.partial(self.query, m, qbuf_next, q_next)]]
         last = None
         for n, b in enumerate(reversed(range(nb))):
+            if n == nb // 2:
+                midway()
             z_ref, p_ref = r.z.at[n % 2], r.p.at[n % 2]
             top = self.scores(b, q_ref, z_ref)
             for f in steps[n]:
@@ -392,7 +410,7 @@
         pltpu.VMEM((2, T, FC), bf16),
         pltpu.VMEM((2, 2) + unit, bf16),
         pltpu.VMEM((3,) + unit, bf16),
-        dma((2,)), dma, dma, dma((5,)), dma((5, d["COLS"] // CHUNK)),
+        dma((2,)), dma, dma, dma((5,)), dma((5, SMALL + (d["COLS"] - SMALL * SMALL_WIDTH) // WIDTH)),
         dma((T // Layer.XB,)), dma((2, 2)), dma((3,)), dma((2,)),
     ]
 
@@ -435,94 +453,97 @@
         for c in copies:
             c.wait()
 
-    groups = d["COLS"] // CHUNK
-    total = groups + LAG[5]
-    first = LAG[5] + 2
-    over_mlp = max(total - first - HEAD_POINTS, 0)
-
-    def head_points(h):
-        return h * HEAD_POINTS // H
-
-    def mlp_points(j):
-        return j * over_mlp // (J - 1)
+    comm = Comm(d, r.stage, r.w, r.send_sem, r.recv_sem)
+    after_heads = FIRST + 2 * H
+    last = comm.groups + LAG[5]
+    over_mlp = last - after_heads
 
     def ready(points):
-        return (points - LAG[5]) * CHUNK
-
-    assert ready(first) >= 2 * HD + 2 * HD
-    assert ready(first) >= 2 * HD + 3 * HD
-    for h in range(H):
-        assert ready(first + head_points(h + 1)) >= min(2 * HD + (h + 2) * 2 * HD + HD, base)
-    assert ready(first + HEAD_POINTS) >= base + 3 * FC
+        return comm.end(max(points - LAG[5], comm.done[5]))
+
+    for k in range(6):
+        assert comm.done[k] >= min(FIRST - LAG[k], comm.groups)
+    assert ready(FIRST) >= 2 * HD + 3 * HD
+    for h in range(1, H):
+        assert ready(FIRST + 2 * h + 1) >= min(2 * HD + (h + 2) * 2 * HD + HD, base)
+    assert ready(FIRST + 2 * H - 1) >= base + 3 * FC
     for j in range(J - 1):
-        assert ready(first + HEAD_POINTS + mlp_points(j + 1)) >= base + (j + 2) * 3 * FC, j
-
+        assert ready(after_heads + (j + 1) * over_mlp // (J - 1)) >= base + (j + 2) * 3 * FC
+
+    arrive(d)
     order_copies(d, r.win, r.wot, r.stage, r.local_sem.at[0])
     for i in range(xbs):
         L.x_copy(i).start()
-    comm = Comm(d, r.stage, r.w, r.send_sem, r.recv_sem)
     own = pltpu.make_async_copy(r.stage, r.w.at[comm.y, comm.x, comm.core], r.local_sem.at[1])
-    meet(d)
-    spread_scale(d, r.ln_tile, r.ln_all, r.ln_send, r.ln_recv)
     pltpu.make_async_copy(r.stage, r.stage, r.local_sem.at[0]).wait()
     own.start()
-    for p in range(LAG[2]):
-        comm.point(p)
-    own.wait()
-    L.tables()
-    L.bias()
-    spread_scale_wait(d, r.ln_all, r.ln_send, r.ln_recv)
-    scale_row(d, r.ln_all, r.ln)
-    per = -(-xbs // (first - 1 - LAG[2]))
-
-    @pl.loop(LAG[2], first)
-    def _(p):
-        with jax.named_scope("point_start"):
-            comm.point(p)
-
-        @pl.loop(0, per)
-        def _(k):
-            i = (p - LAG[2]) * per + k
-
-            @pl.when(i < xbs)
-            def _():
-                L.norm(i)
-
-        @pl.when(p == first - 2)
-        def _():
-            start(fetch_kv())
-
-    start(fetch_q(0))
-    with jax.named_scope("wait_kv"):
-        wait(fetch_kv())
-    L.keys(r.wbuf.at[0, 0], r.wbuf.at[0, 1])
-    pltpu.make_async_copy(r.k, r.kc.at[0], r.csem.at[0]).start()
-    pltpu.make_async_copy(r.v, r.vc.at[0], r.csem.at[1]).start()
-    start(fetch_q(1))
-    start(fetch_o(0))
-    wait(fetch_q(0))
-    for m in range(mbs):
-        L.query(m, r.wbuf.at[1, 0], r.q.at[0])
+    meet(d)
+    normed = keyed = queried = 0
+    for n, (what, g) in enumerate(OPENING):
+        if what <= 5:
+            if (what, g) == (2, 0):
+                own.wait()
+            comm.stage_fn(what, g, g < SMALL)
+            if n == 0:
+                spread_scale(d, r.ln_tile, r.ln_all, r.ln_send, r.ln_recv)
+            if what == 5 and comm.end(g) < 3 * HD <= comm.end(g + 1):
+                start(fetch_kv())
+                start(fetch_q(0))
+            if what == 5 and comm.end(g) < 5 * HD <= comm.end(g + 1):
+                start(fetch_q(1))
+                start(fetch_o(0))
+        elif what == NORM:
+            if normed == 0:
+                L.tables()
+                L.bias()
+                spread_scale_wait(d, r.ln_all, r.ln_send, r.ln_recv)
+                scale_row(d, r.ln_all, r.ln)
+            many = min(g, xbs - normed)
+            if many > 0:
+                @pl.loop(normed, normed + many)
+                def _(i):
+                    L.norm(i)
+            normed += many
+        elif what == KEYS:
+            if keyed == 0:
+                assert normed == xbs
+                wait(fetch_kv())
+            if keyed < mbs:
+                L.keys(keyed, r.wbuf.at[0, 0], r.wbuf.at[0, 1])
+            keyed += 1
+            if keyed == mbs:
+                pltpu.make_async_copy(r.k, r.kc.at[0], r.csem.at[0]).start()
+                pltpu.make_async_copy(r.v, r.vc.at[0], r.csem.at[1]).start()
+        else:
+            if queried == 0:
+                wait(fetch_q(0))
+            for m in range(queried, min(queried + g, mbs)):
+                L.query(m, r.wbuf.at[1, 0], r.q.at[0])
+            queried += g
     r.o[1] = jnp.zeros((d["T"], HD), jnp.bfloat16)
     r.obuf[2] = jnp.zeros(r.obuf.shape[1:], jnp.bfloat16)
 
     @pl.loop(0, H)
     def _(h):
-        lo, hi = lax.div(h * HEAD_POINTS, H), lax.div((h + 1) * HEAD_POINTS, H)
-
-        @pl.loop(first + lo, first + hi)
-        def _(p):
-            with jax.named_scope("point_head"):
-                comm.point(p)
+        with jax.named_scope("point_head"):
+            comm.point(FIRST + 2 * h, FIRST, after_heads)
+
+        @pl.when(h == 1)
+        def _():
+            start(fetch_o(h))
+            start(fetch_q(h + 1))
+
+        @pl.when(jnp.logical_and(h > 0, h + 1 < H))
+        def _():
+            start(fetch_o(h + 1))
+
+        @pl.when(jnp.logical_and(h > 0, h + 2 < H))
+        def _():
+            start(fetch_q(h + 2))
 
         @pl.when(h + 1 < H)
         def _():
             wait(fetch_q(h + 1))
-            start(fetch_o(h + 1))
-
-        @pl.when(h + 2 < H)
-        def _():
-            start(fetch_q(h + 2))
 
         @pl.when(h > 0)
         def _():
@@ -533,21 +554,25 @@
             start(fetch_mlp(0))
 
         s = lax.rem(h, 2)
+
+        def midway():
+            with jax.named_scope("point_mid"):
+                comm.point(FIRST + 2 * h + 1, FIRST, after_heads)
+
         with jax.named_scope("head"):
-            L.head(r.q.at[s], r.o.at[s], r.q.at[1 - s], r.wbuf.at[1, 1 - s], r.o.at[1 - s], r.obuf.at[lax.rem(h + 2, 3)])
+            L.head(r.q.at[s], r.o.at[s], r.q.at[1 - s], r.wbuf.at[1, 1 - s], r.o.at[1 - s], r.obuf.at[lax.rem(h + 2, 3)], midway)
 
     wait(fetch_o(H - 1))
     wait(fetch_mlp(0))
 
-    def mlp_point(j):
-        lo, hi = lax.div(j * over_mlp, J - 1), lax.div((j + 1) * over_mlp, J - 1)
-
-        @pl.loop(first + HEAD_POINTS + lo, first + HEAD_POINTS + hi)
+    def mlp_point(j, lo, hi):
+        @pl.loop(after_heads + lax.div(j * over_mlp, J - 1), after_heads + lax.div((j + 1) * over_mlp, J - 1))
         def _(p):
             with jax.named_scope("point_mlp"):
-                comm.point(p)
-
-    mlp_point(0)
+                comm.point(p, lo, hi)
+
+    opening = after_heads + -(-over_mlp // (J - 1))
+    mlp_point(0, after_heads, opening)
     start(fetch_mlp(1))
     per = tiles // mbs
     for m in range(mbs):
@@ -559,14 +584,13 @@
     def _(j):
         @pl.when(j + 1 < J)
         def _():
-            mlp_point(j)
+            mlp_point(j, after_heads + over_mlp // (J - 1), last)
             start(fetch_mlp(j + 1))
 
         with jax.named_scope("wait_mlp"):
             wait(fetch_mlp(j))
         s = lax.rem(j, 2)
         prev = r.obuf.at[lax.rem(j - 1 + H, 3)]
-        per = tiles // mbs
         with jax.named_scope("mlp"):
             for m in range(mbs):
                 L.gated(m, r.wbuf.at[s, 0], r.wbuf.at[s, 1], r.a.at[s])
@@ -604,7 +628,40 @@
         cost_estimate=pl.CostEstimate(flops=flops, bytes_accessed=4 * T * E + 2 * E * d["COLS"], transcendentals=0),
         name="layer",
     )(ln_tile, w_in, wot, x, prompt_len, rc, rs)
-    return y, kc, vc
+    return hand_on(y, kc, vc)
+
+
+def hand_on_kernel(parts, *refs):
+    n = len(parts)
+    src, dst, buf, sem_in, sem_out = refs[:n], refs[n:2 * n], refs[2 * n:3 * n], refs[3 * n], refs[3 * n + 1]
+    moves = []
+    for i, blocks in enumerate(parts):
+        rows = src[i].shape[1] // blocks
+        for k in range(blocks):
+            at = pl.ds(k * rows, rows)
+            moves.append((src[i].at[0, at, :], buf[i].at[at, :], dst[i].at[0, at, :]))
+    for k, (a, b, _) in enumerate(moves):
+        pltpu.make_async_copy(a, b, sem_in.at[k]).start()
+    for k, (a, b, c) in enumerate(moves):
+        pltpu.make_async_copy(a, b, sem_in.at[k]).wait()
+        pltpu.make_async_copy(b, c, sem_out.at[k]).start()
+    for k, (_, b, c) in enumerate(moves):
+        pltpu.make_async_copy(b, c, sem_out.at[k]).wait()
+
+
+def hand_on(y, kc, vc):
+    arrays, parts = (y, kc, vc), (8, 1, 1)
+    hbm = pl.BlockSpec(memory_space=HBM)
+    return pl.pallas_call(
+        functools.partial(hand_on_kernel, parts),
+        out_shape=tuple(jax.ShapeDtypeStruct(a.shape, a.dtype) for a in arrays),
+        in_specs=[hbm] * 3,
+        out_specs=(hbm,) * 3,
+        scratch_shapes=[pltpu.VMEM(a.shape[1:], a.dtype) for a in arrays]
+        + [pltpu.SemaphoreType.DMA((sum(parts),)), pltpu.SemaphoreType.DMA((sum(parts),))],
+        compiler_params=pltpu.CompilerParams(vmem_limit_bytes=VMEM_LIMIT),
+        name="hand_on",
+    )(*arrays)
 
 
 def solution(mesh):

time: 388 us -> 377 us (0.972)
  local copies, waits for them, and re-layouts: 11.9 us -> 1.34 us
    unnamed x7 -> x0, local copies, waits for them, and re-layouts: 10.5 us -> none
    pallas_call x1, Pallas kernels: 375 us -> 366 us  [layer(): pl.pallas_call(functools.partial(kernel, d), out_shape=(jax.ShapeDtypeStr...]
    pallas_call x0 -> x1, Pallas kernels: none -> 8.19 us  [hand_on(): pl.pallas_call(functools.partial(hand_on_kernel, parts), out_shape=tuple(...]
where the time goes in v4:
time: 377 us
  Pallas kernels  374 us (99%)
    pallas_call x1, Pallas kernels, layer(): pl.pallas_call(functools.partial(kernel, d), out_shape=(jax.ShapeDtypeStr...  366 us
    pallas_call x1, Pallas kernels, hand_on(): pl.pallas_call(functools.partial(hand_on_kernel, parts), out_shape=tuple(...  8.19 us

profile of v4, /device:TPU:96, one launch (start us, length us, event | category | flops | bytes accessed | tf_op | source)
XLA Modules:
  0.0 377.2 jit_solution(9997689999168302899)
XLA Ops:
  1.3 0.7 tile.2
  1.9 0.1 broadcast_in_dim.7
  2.0 0.6 broadcast_in_dim.8.refs_0_
  2.6 366.2 %layer.1 = (bf16[1,2048,2048]{2,1,0:T(8,128)(2,1)}, bf16[1,2048,256]{2,1,0:T(8,128)(2,1)}, bf16[1,2048,256]{2,1,0:T(8,128)(2,1)}, bf16[4,4,2,64,29184]{4,3,2,1,0:T(8,128)(2,1)}) custom-call(f32[8,128]{1,0:T(8,128)} %broadcast_in_dim.8.refs_0_, bf16[64,18944]{1,0:T(8,128)(2,1)} %refs_1_.1, bf16[64,10240]{1,0:T(8,128)(2,1)} %bitcast.1, ...), custom_call_target="tpu_custom_call" | custom-call | flops 261993005056 | bytes 136314880 | tf_op jit(solution)/shard_map/layer/pallas_call | solution.py:620
  368.8 8.2 %hand_on.1 = (bf16[1,2048,2048]{2,1,0:T(8,128)(2,1)}, bf16[1,2048,256]{2,1,0:T(8,128)(2,1)}, bf16[1,2048,256]{2,1,0:T(8,128)(2,1)}) custom-call(bf16[1,2048,2048]{2,1,0:T(8,128)(2,1)} %get-tuple-element.6.refs_0_, bf16[1,2048,256]{2,1,0:T(8,128)(2,1)} %get-tuple-element.7.refs_1_, bf16[1,2048,256]{2,1,0:T(8,128)(2,1)} %get-tuple-element.8.refs_2_), custom_call_target="tpu_custom_call" | custom-call | tf_op jit(solution)/shard_map/hand_on/pallas_call | solution.py:655

commit v5 on v4

--- a/solution.py
+++ b/solution.py
@@ -19,13 +19,10 @@
 SMALL, SMALL_WIDTH, WIDTH = 20, 384, 768
 LAG = (0, 2, 4, 6, 8, 9)
 FIRST = 12
-NORM, KEYS, QUERY = 6, 7, 8
-OPENING = (
-    (0, 0), (0, 1), (0, 2), (0, 3), (0, 4), (0, 5), (0, 6), (1, 0), (1, 1), (0, 7), (1, 2), (1, 3), (0, 8), (1, 4),
-    (NORM, 2), (1, 5), (NORM, 1), (1, 6), (NORM, 1), (2, 0), (2, 1), (NORM, 11), (1, 7), (NORM, 1), (1, 8), (0, 9),
-    (3, 0), (2, 2), (3, 1), (2, 3), (4, 0), (1, 9), (0, 10), (3, 2), (2, 4), (4, 1), (5, 0), (3, 3), (2, 5), (5, 1),
-    (KEYS, 1), (4, 2), (KEYS, 1), (1, 10), (4, 3), (KEYS, 1), (3, 4), (2, 6), (KEYS, 1), (5, 2), (3, 5), (2, 7),
-    (QUERY, 2), (5, 3), (QUERY, 2), (0, 11))
+KEYS, QUERY, NORM = 6, 7, 8
+OPENING = (0, 0, 0, 0, 0, 0, 0, 1, 1, 0, 1, 1, 0, 1, NORM + 2, 1, NORM + 1, 1, NORM + 1, 2, 2, NORM + 11, 1, NORM + 1, 1, 0,
+           3, 2, 3, 2, 4, 1, 0, 3, 2, 4, 5, 3, 2, 5, KEYS, 4, KEYS, 1, 4, KEYS, 3, 2, KEYS, 5, 3, 2,
+           QUERY, QUERY, 5, QUERY, QUERY, 0)
 
 
 def dims(mesh, x, w_in, w_out):
@@ -44,31 +41,32 @@
     return lax.axis_index("d")
 
 
-def order_copies(d, win_ref, wot_ref, stage_ref, sem):
+def order_copies(d, win_ref, wot_ref, stage_ref, sem, part):
     F, H, HD, FC = d["F"], d["H"], d["HD"], d["FC"]
     qs = 2 * F
     ks = qs + H * HD
-    pltpu.make_async_copy(win_ref.at[:, pl.ds(ks, 2 * HD)], stage_ref.at[:, pl.ds(0, 2 * HD)], sem).start()
-
-    @pl.loop(0, H)
-    def _(h):
-        at = pl.multiple_of(2 * HD + h * 2 * HD, HD)
-        pltpu.make_async_copy(win_ref.at[:, pl.ds(pl.multiple_of(qs + h * HD, HD), HD)],
-                              stage_ref.at[:, pl.ds(at, HD)], sem).start()
-        pltpu.make_async_copy(wot_ref.at[:, pl.ds(pl.multiple_of(F + h * HD, HD), HD)],
-                              stage_ref.at[:, pl.ds(at + HD, HD)], sem).start()
-
     base = 2 * HD + H * 2 * HD
+
+    def move(src_ref, col, at, width, which):
+        pltpu.make_async_copy(src_ref.at[:, pl.ds(pl.multiple_of(col, HD), width)],
+                              stage_ref.at[:, pl.ds(pl.multiple_of(at, HD), width)], sem.at[which]).start()
+
+    if part == 0:
+        move(win_ref, ks, 0, 2 * HD, 0)
+
+        @pl.loop(0, H)
+        def _(h):
+            move(win_ref, qs + h * HD, 2 * HD + h * 2 * HD, HD, 0)
+            move(wot_ref, F + h * HD, 3 * HD + h * 2 * HD, HD, 0)
+
+        return
 
     @pl.loop(0, F // FC)
     def _(j):
-        at = pl.multiple_of(base + j * 3 * FC, FC)
-        pltpu.make_async_copy(win_ref.at[:, pl.ds(pl.multiple_of(j * FC, FC), FC)],
-                              stage_ref.at[:, pl.ds(at, FC)], sem).start()
-        pltpu.make_async_copy(win_ref.at[:, pl.ds(pl.multiple_of(F + j * FC, FC), FC)],
-                              stage_ref.at[:, pl.ds(at + FC, FC)], sem).start()
-        pltpu.make_async_copy(wot_ref.at[:, pl.ds(pl.multiple_of(j * FC, FC), FC)],
-                              stage_ref.at[:, pl.ds(at + 2 * FC, FC)], sem).start()
+        at = base + j * 3 * FC
+        move(win_ref, j * FC, at, FC, 1)
+        move(win_ref, F + j * FC, at + FC, FC, 1)
+        move(wot_ref, j * FC, at + 2 * FC, FC, 1)
 
 
 class Comm:
@@ -76,7 +74,7 @@
         self.d = d
         self.stage, self.w, self.send, self.recv = stage_ref, w_ref, send_sem, recv_sem
         self.groups = SMALL + (d["COLS"] - SMALL * SMALL_WIDTH) // WIDTH
-        self.done = [sum(1 for op in OPENING if op[0] == k) for k in range(6)]
+        self.done = [OPENING.count(k) for k in range(6)]
         side, cores = d["SIDE"], d["CORES"]
         me = place()
         self.core = lax.rem(me, cores)
@@ -195,13 +193,9 @@
 
 
 def scale_row(d, ln_all, row_ref):
-    lane = lax.broadcasted_iota(jnp.int32, (1, 128), 1)
     per = 128 // d["R"]
     for i in range(d["E"] // 128):
-        part = ln_all[per * i][0:1, :]
-        for k in range(1, per):
-            part = jnp.where(lane < k * d["R"], part, ln_all[per * i + k][0:1, :])
-        row_ref[0:1, i * 128:(i + 1) * 128] = part
+        row_ref[0:1, i * 128:(i + 1) * 128] = jnp.concatenate([ln_all[per * i + k] for k in range(per)], axis=1)
 
 
 def nn(a, b):
@@ -230,9 +224,9 @@
         rows = pl.ds(pl.multiple_of(i * self.XB, self.XB), self.XB)
         return pltpu.make_async_copy(self.r.x.at[0, rows, :], self.r.h.at[rows, :], self.r.xsem.at[i])
 
-    def y_copy(self, m):
-        rows = pl.ds(m * self.MB, self.MB)
-        return pltpu.make_async_copy(self.r.h.at[rows, :], self.r.y.at[0, rows, :], self.r.xsem.at[m])
+    def y_copy(self, t):
+        cols = pl.ds(t * self.d["FC"], self.d["FC"])
+        return pltpu.make_async_copy(self.r.h.at[:, cols], self.r.y.at[0, :, cols], self.r.xsem.at[t])
 
     def unit(self, col, buf, sem):
         return pltpu.make_async_copy(self.r.w.at[:, :, :, :, pl.ds(pl.multiple_of(col, 128), self.d["FC"])], buf, sem)
@@ -366,24 +360,22 @@
     def finish(self, a_ref, obuf):
         d, r = self.d, self.r
         fc = d["FC"]
-        for m in range(d["T"] // self.MB):
-            rows = slice(m * self.MB, (m + 1) * self.MB)
-            for t in range(d["E"] // fc):
-                cols = slice(t * fc, (t + 1) * fc)
-                total = r.yacc[rows, cols] + nt(a_ref[rows, :], self.wval(obuf)[cols, :])
-                r.h[rows, cols] = total.astype(jnp.bfloat16)
-            self.y_copy(m).start()
-        for m in range(d["T"] // self.MB):
-            self.y_copy(m).wait()
+        for t in range(d["E"] // fc):
+            cols = slice(t * fc, (t + 1) * fc)
+            total = r.yacc[:, cols] + nt(a_ref[...], self.wval(obuf)[cols, :])
+            r.h[:, cols] = total.astype(jnp.bfloat16)
+            self.y_copy(t).start()
+        for t in range(d["E"] // fc):
+            self.y_copy(t).wait()
 
 
 class Refs:
     pass
 
 
-NAMES = ("ln_tile", "win", "wot", "x", "plen", "rc", "rs",
+NAMES = ("ln_own", "win", "wot", "x", "plen", "rc", "rs",
          "y", "kc", "vc", "w",
-         "stage", "ln_all", "ln", "h", "yacc", "cos", "sin", "bias", "k", "kt", "v", "q", "o", "z", "p", "a", "wbuf", "obuf",
+         "stage", "ln_all", "ln", "h", "yacc", "cos", "sin", "bias", "k", "kt", "v", "q", "z", "p", "a", "wbuf", "obuf",
          "local_sem", "ln_send", "ln_recv", "send_sem", "recv_sem", "xsem", "wsem", "osem", "csem")
 
 
@@ -393,7 +385,7 @@
     bf16, f32, dma = jnp.bfloat16, jnp.float32, pltpu.SemaphoreType.DMA
     return [
         pltpu.VMEM((d["R"], d["COLS"]), bf16),
-        pltpu.VMEM((d["D"], 8, 128), f32),
+        pltpu.VMEM((d["D"], 1, d["R"]), f32),
         pltpu.VMEM((1, E), f32),
         pltpu.VMEM((T, E), bf16),
         pltpu.VMEM((T, E), f32),
@@ -404,14 +396,13 @@
         pltpu.VMEM((HD, T), bf16),
         pltpu.VMEM((T, HD), bf16),
         pltpu.VMEM((2, T, HD), bf16),
-        pltpu.VMEM((2, T, HD), bf16),
         pltpu.VMEM((2, Layer.QB, T), f32),
         pltpu.VMEM((2, Layer.QB, T), bf16),
         pltpu.VMEM((2, T, FC), bf16),
         pltpu.VMEM((2, 2) + unit, bf16),
         pltpu.VMEM((3,) + unit, bf16),
-        dma((2,)), dma, dma, dma((5,)), dma((5, SMALL + (d["COLS"] - SMALL * SMALL_WIDTH) // WIDTH)),
-        dma((T // Layer.XB,)), dma((2, 2)), dma((3,)), dma((2,)),
+        dma((4,)), dma, dma, dma((5,)), dma((5, SMALL + (d["COLS"] - SMALL * SMALL_WIDTH) // WIDTH)),
+        dma((max(T // Layer.XB, E // FC),)), dma((2, 2)), dma((3,)), dma((2,)),
     ]
 
 
@@ -470,57 +461,100 @@
     for j in range(J - 1):
         assert ready(after_heads + (j + 1) * over_mlp // (J - 1)) >= base + (j + 2) * 3 * FC
 
+    mine = r.w.at[comm.y, comm.x, comm.core]
+    early, late = pl.ds(0, base), pl.ds(base, d["COLS"] - base)
+    own = [pltpu.make_async_copy(r.stage.at[:, part], mine.at[:, part], r.local_sem.at[2 + i])
+           for i, part in enumerate((early, late))]
+    rest = r.stage.at[:, late]
+    order_copies(d, r.win, r.wot, r.stage, r.local_sem, 0)
     arrive(d)
-    order_copies(d, r.win, r.wot, r.stage, r.local_sem.at[0])
     for i in range(xbs):
         L.x_copy(i).start()
-    own = pltpu.make_async_copy(r.stage, r.w.at[comm.y, comm.x, comm.core], r.local_sem.at[1])
-    pltpu.make_async_copy(r.stage, r.stage, r.local_sem.at[0]).wait()
-    own.start()
+    pltpu.make_async_copy(r.stage.at[:, early], r.stage.at[:, early], r.local_sem.at[0]).wait()
+    own[0].start()
     meet(d)
+    reached = set()
+
+    def late_begun():
+        if "begun" not in reached:
+            reached.add("begun")
+            order_copies(d, r.win, r.wot, r.stage, r.local_sem, 1)
+
+    def late_ready():
+        late_begun()
+        if "late" not in reached:
+            reached.add("late")
+            pltpu.make_async_copy(rest, rest, r.local_sem.at[1]).wait()
+            own[1].start()
+
+    def late_placed():
+        late_ready()
+        if "placed" not in reached:
+            reached.add("placed")
+            own[1].wait()
+
     normed = keyed = queried = 0
-    for n, (what, g) in enumerate(OPENING):
+    next_group = [0] * 6
+    for what in OPENING:
         if what <= 5:
+            g = next_group[what]
+            next_group[what] += 1
             if (what, g) == (2, 0):
-                own.wait()
-            comm.stage_fn(what, g, g < SMALL)
-            if n == 0:
-                spread_scale(d, r.ln_tile, r.ln_all, r.ln_send, r.ln_recv)
+                own[0].wait()
+            if what == 0 and comm.end(g + 1) > base:
+                late_ready()
+            if what == 2 and comm.end(g + 1) > base:
+                late_placed()
+            with jax.named_scope(f"stage{what}"):
+                comm.stage_fn(what, g, g < SMALL)
+            if (what, g) == (0, 1):
+                spread_scale(d, r.ln_own, r.ln_all, r.ln_send, r.ln_recv)
+            if what == 1:
+                late_begun()
             if what == 5 and comm.end(g) < 3 * HD <= comm.end(g + 1):
                 start(fetch_kv())
                 start(fetch_q(0))
             if what == 5 and comm.end(g) < 5 * HD <= comm.end(g + 1):
                 start(fetch_q(1))
                 start(fetch_o(0))
-        elif what == NORM:
-            if normed == 0:
-                L.tables()
-                L.bias()
-                spread_scale_wait(d, r.ln_all, r.ln_send, r.ln_recv)
-                scale_row(d, r.ln_all, r.ln)
-            many = min(g, xbs - normed)
-            if many > 0:
-                @pl.loop(normed, normed + many)
-                def _(i):
-                    L.norm(i)
-            normed += many
         elif what == KEYS:
             if keyed == 0:
                 assert normed == xbs
-                wait(fetch_kv())
+                with jax.named_scope("wait_kv"):
+                    wait(fetch_kv())
             if keyed < mbs:
-                L.keys(keyed, r.wbuf.at[0, 0], r.wbuf.at[0, 1])
+                with jax.named_scope("keys"):
+                    L.keys(keyed, r.wbuf.at[0, 0], r.wbuf.at[0, 1])
             keyed += 1
             if keyed == mbs:
                 pltpu.make_async_copy(r.k, r.kc.at[0], r.csem.at[0]).start()
                 pltpu.make_async_copy(r.v, r.vc.at[0], r.csem.at[1]).start()
-        else:
+        elif what == QUERY:
             if queried == 0:
                 wait(fetch_q(0))
-            for m in range(queried, min(queried + g, mbs)):
-                L.query(m, r.wbuf.at[1, 0], r.q.at[0])
-            queried += g
-    r.o[1] = jnp.zeros((d["T"], HD), jnp.bfloat16)
+            if queried < mbs:
+                with jax.named_scope("query"):
+                    L.query(queried, r.wbuf.at[1, 0], r.q.at[0])
+            queried += 1
+        else:
+            if normed == 0:
+                late_ready()
+                with jax.named_scope("tables"):
+                    L.tables()
+                    L.bias()
+                with jax.named_scope("wait_scale"):
+                    spread_scale_wait(d, r.ln_all, r.ln_send, r.ln_recv)
+                    scale_row(d, r.ln_all, r.ln)
+            many = min(what - NORM, xbs - normed)
+            if many > 0:
+                with jax.named_scope("norm"):
+                    @pl.loop(normed, normed + many)
+                    def _(i):
+                        L.norm(i)
+            normed += many
+    late_ready()
+    late_placed()
+    r.a[1] = jnp.zeros((d["T"], FC), jnp.bfloat16)
     r.obuf[2] = jnp.zeros(r.obuf.shape[1:], jnp.bfloat16)
 
     @pl.loop(0, H)
@@ -560,37 +594,26 @@
                 comm.point(FIRST + 2 * h + 1, FIRST, after_heads)
 
         with jax.named_scope("head"):
-            L.head(r.q.at[s], r.o.at[s], r.q.at[1 - s], r.wbuf.at[1, 1 - s], r.o.at[1 - s], r.obuf.at[lax.rem(h + 2, 3)], midway)
+            L.head(r.q.at[s], r.a.at[s], r.q.at[1 - s], r.wbuf.at[1, 1 - s], r.a.at[1 - s], r.obuf.at[lax.rem(h + 2, 3)], midway)
 
     wait(fetch_o(H - 1))
-    wait(fetch_mlp(0))
-
-    def mlp_point(j, lo, hi):
-        @pl.loop(after_heads + lax.div(j * over_mlp, J - 1), after_heads + lax.div((j + 1) * over_mlp, J - 1))
-        def _(p):
-            with jax.named_scope("point_mlp"):
-                comm.point(p, lo, hi)
-
-    opening = after_heads + -(-over_mlp // (J - 1))
-    mlp_point(0, after_heads, opening)
-    start(fetch_mlp(1))
-    per = tiles // mbs
-    for m in range(mbs):
-        L.gated(m, r.wbuf.at[0, 0], r.wbuf.at[0, 1], r.a.at[0])
-        for t in range(m * per, (m + 1) * per):
-            L.add_out(r.o.at[(H - 1) % 2], r.obuf.at[(H - 1) % 3], t)
-
-    @pl.loop(1, J)
+
+    @pl.loop(0, J)
     def _(j):
         @pl.when(j + 1 < J)
         def _():
-            mlp_point(j, after_heads + over_mlp // (J - 1), last)
+            @pl.loop(after_heads + lax.div(j * over_mlp, J - 1), after_heads + lax.div((j + 1) * over_mlp, J - 1))
+            def _(p):
+                with jax.named_scope("point_mlp"):
+                    comm.point(p, after_heads, last)
+
             start(fetch_mlp(j + 1))
 
         with jax.named_scope("wait_mlp"):
             wait(fetch_mlp(j))
         s = lax.rem(j, 2)
         prev = r.obuf.at[lax.rem(j - 1 + H, 3)]
+        per = tiles // mbs
         with jax.named_scope("mlp"):
             for m in range(mbs):
                 L.gated(m, r.wbuf.at[s, 0], r.wbuf.at[s, 1], r.a.at[s])
@@ -612,7 +635,6 @@
     angles = steps[:, None] * inv_freq[None, :]
     rc = jnp.asarray(np.cos(angles), jnp.float32)
     rs = jnp.asarray(np.sin(angles), jnp.float32)
-    ln_tile = jnp.broadcast_to(jnp.tile(ln, 128 // d["R"])[None], (8, 128))
     w_shape = (d["SIDE"], d["SIDE"], d["CORES"], d["R"], d["COLS"])
     hbm, vmem = pl.BlockSpec(memory_space=HBM), pl.BlockSpec(memory_space=pltpu.VMEM)
     flops = 2 * T * E * d["COLS"] + 2 * T * T * HD * d["H"]
@@ -627,7 +649,7 @@
         compiler_params=pltpu.CompilerParams(collective_id=0, has_side_effects=True, vmem_limit_bytes=VMEM_LIMIT),
         cost_estimate=pl.CostEstimate(flops=flops, bytes_accessed=4 * T * E + 2 * E * d["COLS"], transcendentals=0),
         name="layer",
-    )(ln_tile, w_in, wot, x, prompt_len, rc, rs)
+    )(ln[None], w_in, wot, x, prompt_len, rc, rs)
     return hand_on(y, kc, vc)
 
 

time: 377 us -> 375 us (level)
  no operation moved by 1% of the time
where the time goes in v5:
time: 375 us
  Pallas kernels  374 us (100%)
    pallas_call x1, Pallas kernels, layer(): pl.pallas_call(functools.partial(kernel, d), out_shape=(jax.ShapeDtypeStr...  366 us
    pallas_call x1, Pallas kernels, hand_on(): pl.pallas_call(functools.partial(hand_on_kernel, parts), out_shape=tuple(...  8.19 us

profile of v5, /device:TPU:96, one launch (start us, length us, event | category | flops | bytes accessed | tf_op | source)
XLA Modules:
  0.0 375.2 jit_solution(4073153840056968523)
XLA Ops:
  1.3 365.5 %layer.1 = (bf16[1,2048,2048]{2,1,0:T(8,128)(2,1)}, bf16[1,2048,256]{2,1,0:T(8,128)(2,1)}, bf16[1,2048,256]{2,1,0:T(8,128)(2,1)}, bf16[4,4,2,64,29184]{4,3,2,1,0:T(8,128)(2,1)}) custom-call(f32[1,64]{1,0:T(1,128)} %bitcast.3, bf16[64,18944]{1,0:T(8,128)(2,1)} %refs_1_.1, bf16[64,10240]{1,0:T(8,128)(2,1)} %bitcast.2, bf16[1,2048,2048]{2,1,0:T(8,128)(2,1)} %refs_3_.1, ...), custom_call_target="tpu_custom_call" | custom-call | flops 261993005056 | bytes 136314880 | tf_op jit(solution)/shard_map/layer/pallas_call | solution.py:642
  366.8 8.2 %hand_on.1 = (bf16[1,2048,2048]{2,1,0:T(8,128)(2,1)}, bf16[1,2048,256]{2,1,0:T(8,128)(2,1)}, bf16[1,2048,256]{2,1,0:T(8,128)(2,1)}) custom-call(bf16[1,2048,2048]{2,1,0:T(8,128)(2,1)} %get-tuple-element.6.refs_0_, bf16[1,2048,256]{2,1,0:T(8,128)(2,1)} %get-tuple-element.7.refs_1_, bf16[1,2048,256]{2,1,0:T(8,128)(2,1)} %get-tuple-element.8.refs_2_), custom_call_target="tpu_custom_call" | custom-call | tf_op jit(solution)/shard_map/hand_on/pallas_call | solution.py:677

commit v6 on v5

--- a/solution.py
+++ b/solution.py
@@ -16,13 +16,14 @@
 HBM = pltpu.HBM
 VMEM_LIMIT = 67043328
 
-SMALL, SMALL_WIDTH, WIDTH = 20, 384, 768
+SMALL, SMALL_WIDTH, WIDTH = 10, 384, 768
 LAG = (0, 2, 4, 6, 8, 9)
 FIRST = 12
+EARLY = 3
 KEYS, QUERY, NORM = 6, 7, 8
-OPENING = (0, 0, 0, 0, 0, 0, 0, 1, 1, 0, 1, 1, 0, 1, NORM + 2, 1, NORM + 1, 1, NORM + 1, 2, 2, NORM + 11, 1, NORM + 1, 1, 0,
-           3, 2, 3, 2, 4, 1, 0, 3, 2, 4, 5, 3, 2, 5, KEYS, 4, KEYS, 1, 4, KEYS, 3, 2, KEYS, 5, 3, 2,
-           QUERY, QUERY, 5, QUERY, QUERY, 0)
+OPENING = (0, 0, 0, 0, 0, 0, 0, 0, 1, 1, 0, 1, 1, 0, 1, NORM + 1, 1, 0, NORM + 3, 1, NORM + 1, 2, 2, NORM + 11, 1, 1, 1, 1,
+           3, 2, 3, 2, 4, 0, 3, 2, 4, 5, 3, 2, 5, KEYS, 4, KEYS, 3, 2, KEYS, 4, KEYS, 5, 1, QUERY, 3, 2, QUERY, QUERY, 4,
+           QUERY, 5)
 
 
 def dims(mesh, x, w_in, w_out):
@@ -131,11 +132,12 @@
                 self.put(b, b, 2, g, self.dev(y, self.wrap(x + s), c)).start()
         elif stage == 3:
             self.landed(w.at[0:2, :, :, ra, cols], 2, g)
-            ys, xs = self.wrap(y - turn), self.wrap(x + turn)
-            a = w.at[ys, :, c, ra, cols]
-            self.put(a, a, 3, g, self.dev(self.wrap(y + turn), x, c)).start()
-            b = w.at[:, xs, c, rb, cols]
-            self.put(b, b, 3, g, self.dev(y, self.wrap(x - turn), c)).start()
+            quarter = half // 2
+            for i, s in enumerate((1, -1)):
+                a = w.at[self.wrap(y - s), :, c, pl.ds(i * quarter, quarter), cols]
+                self.put(a, a, 3, g, self.dev(self.wrap(y + s), x, c)).start()
+                b = w.at[:, self.wrap(x - s), c, pl.ds(half + i * quarter, quarter), cols]
+                self.put(b, b, 3, g, self.dev(y, self.wrap(x + s), c)).start()
         elif stage == 4:
             self.landed(w.at[0, :, :, ra, cols], 3, g)
             a = w.at[:, :, c, :, cols]
@@ -445,21 +447,24 @@
             c.wait()
 
     comm = Comm(d, r.stage, r.w, r.send_sem, r.recv_sem)
-    after_heads = FIRST + 2 * H
+    after_early = FIRST + 2 * EARLY
     last = comm.groups + LAG[5]
-    over_mlp = last - after_heads
+    rest_points, rest_steps = last - after_early, H - EARLY + J - 1
 
     def ready(points):
         return comm.end(max(points - LAG[5], comm.done[5]))
+
+    def points_before(step):
+        return after_early + (lax.div(step * rest_points, rest_steps) if not isinstance(step, int) else step * rest_points // rest_steps)
 
     for k in range(6):
         assert comm.done[k] >= min(FIRST - LAG[k], comm.groups)
     assert ready(FIRST) >= 2 * HD + 3 * HD
     for h in range(1, H):
-        assert ready(FIRST + 2 * h + 1) >= min(2 * HD + (h + 2) * 2 * HD + HD, base)
-    assert ready(FIRST + 2 * H - 1) >= base + 3 * FC
+        had = FIRST + 2 * h + 1 if h < EARLY else points_before(h - EARLY + 1)
+        assert ready(had) >= (min(2 * HD + (h + 2) * 2 * HD + HD, base) if h + 1 < H else base + 3 * FC)
     for j in range(J - 1):
-        assert ready(after_heads + (j + 1) * over_mlp // (J - 1)) >= base + (j + 2) * 3 * FC
+        assert ready(points_before(H - EARLY + j + 1)) >= base + (j + 2) * 3 * FC
 
     mine = r.w.at[comm.y, comm.x, comm.core]
     early, late = pl.ds(0, base), pl.ds(base, d["COLS"] - base)
@@ -559,8 +564,17 @@
 
     @pl.loop(0, H)
     def _(h):
-        with jax.named_scope("point_head"):
-            comm.point(FIRST + 2 * h, FIRST, after_heads)
+        @pl.when(h < EARLY)
+        def _():
+            with jax.named_scope("point_head"):
+                comm.point(FIRST + 2 * h, FIRST, after_early)
+
+        @pl.when(h >= EARLY)
+        def _():
+            @pl.loop(points_before(h - EARLY), points_before(h - EARLY + 1))
+            def _(p):
+                with jax.named_scope("point_head"):
+                    comm.point(p, after_early, points_before(H - EARLY) + 1)
 
         @pl.when(h == 1)
         def _():
@@ -590,8 +604,10 @@
         s = lax.rem(h, 2)
 
         def midway():
-            with jax.named_scope("point_mid"):
-                comm.point(FIRST + 2 * h + 1, FIRST, after_heads)
+            @pl.when(h < EARLY)
+            def _():
+                with jax.named_scope("point_mid"):
+                    comm.point(FIRST + 2 * h + 1, FIRST + 1, after_early)
 
         with jax.named_scope("head"):
             L.head(r.q.at[s], r.a.at[s], r.q.at[1 - s], r.wbuf.at[1, 1 - s], r.a.at[1 - s], r.obuf.at[lax.rem(h + 2, 3)], midway)
@@ -602,10 +618,10 @@
     def _(j):
         @pl.when(j + 1 < J)
         def _():
-            @pl.loop(after_heads + lax.div(j * over_mlp, J - 1), after_heads + lax.div((j + 1) * over_mlp, J - 1))
+            @pl.loop(points_before(H - EARLY + j), points_before(H - EARLY + j + 1))
             def _(p):
                 with jax.named_scope("point_mlp"):
-                    comm.point(p, after_heads, last)
+                    comm.point(p, points_before(H - EARLY), last)
 
             start(fetch_mlp(j + 1))
 

time: 375 us -> 370 us (0.987)
  Pallas kernels: 374 us -> 369 us
    pallas_call x1, Pallas kernels: 366 us -> 361 us  [layer(): pl.pallas_call(functools.partial(kernel, d), out_shape=(jax.ShapeDtypeStr...]
where the time goes in v6:
time: 370 us
  Pallas kernels  369 us (100%)
    pallas_call x1, Pallas kernels, layer(): pl.pallas_call(functools.partial(kernel, d), out_shape=(jax.ShapeDtypeStr...  361 us
    pallas_call x1, Pallas kernels, hand_on(): pl.pallas_call(functools.partial(hand_on_kernel, parts), out_shape=tuple(...  8.19 us

profile of v6, /device:TPU:96, one launch (start us, length us, event | category | flops | bytes accessed | tf_op | source)
XLA Modules:
  0.0 370.2 jit_solution(5900483423853059339)
XLA Ops:
  1.3 360.6 %layer.1 = (bf16[1,2048,2048]{2,1,0:T(8,128)(2,1)}, bf16[1,2048,256]{2,1,0:T(8,128)(2,1)}, bf16[1,2048,256]{2,1,0:T(8,128)(2,1)}, bf16[4,4,2,64,29184]{4,3,2,1,0:T(8,128)(2,1)}) custom-call(f32[1,64]{1,0:T(1,128)} %bitcast.3, bf16[64,18944]{1,0:T(8,128)(2,1)} %refs_1_.1, bf16[64,10240]{1,0:T(8,128)(2,1)} %bitcast.2, bf16[1,2048,2048]{2,1,0:T(8,128)(2,1)} %refs_3_.1, ...), custom_call_target="tpu_custom_call" | custom-call | flops 261993005056 | bytes 136314880 | tf_op jit(solution)/shard_map/layer/pallas_call | solution.py:658
  361.9 8.2 %hand_on.1 = (bf16[1,2048,2048]{2,1,0:T(8,128)(2,1)}, bf16[1,2048,256]{2,1,0:T(8,128)(2,1)}, bf16[1,2048,256]{2,1,0:T(8,128)(2,1)}) custom-call(bf16[1,2048,2048]{2,1,0:T(8,128)(2,1)} %get-tuple-element.6.refs_0_, bf16[1,2048,256]{2,1,0:T(8,128)(2,1)} %get-tuple-element.7.refs_1_, bf16[1,2048,256]{2,1,0:T(8,128)(2,1)} %get-tuple-element.8.refs_2_), custom_call_target="tpu_custom_call" | custom-call | tf_op jit(solution)/shard_map/hand_on/pallas_call | solution.py:693

commit v7 on v6

--- a/solution.py
+++ b/solution.py
@@ -20,10 +20,10 @@
 LAG = (0, 2, 4, 6, 8, 9)
 FIRST = 12
 EARLY = 3
-KEYS, QUERY, NORM = 6, 7, 8
-OPENING = (0, 0, 0, 0, 0, 0, 0, 0, 1, 1, 0, 1, 1, 0, 1, NORM + 1, 1, 0, NORM + 3, 1, NORM + 1, 2, 2, NORM + 11, 1, 1, 1, 1,
-           3, 2, 3, 2, 4, 0, 3, 2, 4, 5, 3, 2, 5, KEYS, 4, KEYS, 3, 2, KEYS, 4, KEYS, 5, 1, QUERY, 3, 2, QUERY, QUERY, 4,
-           QUERY, 5)
+KEYS, QUERY, SCALE, NORM = 6, 7, 8, 9
+OPENING = (SCALE, 0, 0, 0, 0, 0, 0, 0, 0, SCALE, 1, 1, SCALE, 0, 1, 1, SCALE, 0, 1, 1, SCALE, 0, 1, 2, 2, NORM + 12, 1, 1,
+           NORM + 1, 1, 1, NORM + 3, 3, 2, 3, 2, 4, 0, 3, 2, 4, 5, 3, 2, 5, KEYS, 4, KEYS, 3, 2, KEYS, 4, KEYS, 5, 1, QUERY,
+           3, 2, QUERY, QUERY, 4, QUERY, 5)
 
 
 def dims(mesh, x, w_in, w_out):
@@ -89,6 +89,11 @@
     def dev(self, y, x, core):
         d = self.d
         return {"d": (y * d["SIDE"] + x) * d["CORES"] + core}
+
+    def near(self):
+        ways = [self.dev(self.y, self.wrap(self.x + s), self.core) for s in (1, -1)]
+        ways += [self.dev(self.wrap(self.y + s), self.x, self.core) for s in (1, -1)]
+        return ways + [self.dev(self.y, self.x, 1 - self.core)]
 
     def wrap(self, v):
         side = self.d["SIDE"]
@@ -164,40 +169,53 @@
             pltpu.make_async_copy(ref, ref, self.send.at[stage]).wait()
 
 
-def arrive(d):
+def arrive(comm):
     barrier = pltpu.get_barrier_semaphore()
-    me = place()
-
-    @pl.loop(1, d["D"])
-    def _(i):
-        pl.semaphore_signal(barrier, inc=1, device_id={"d": lax.rem(me + i, d["D"])}, device_id_type=MESH)
-
-
-def meet(d):
-    pl.semaphore_wait(pltpu.get_barrier_semaphore(), d["D"] - 1)
-
-
-def spread_scale(d, ln_ref, ln_all, ln_send, ln_recv):
-    me = place()
-
-    @pl.loop(1, d["D"])
-    def _(i):
-        pltpu.make_async_remote_copy(src_ref=ln_ref, dst_ref=ln_all.at[me], send_sem=ln_send, recv_sem=ln_recv,
-                                     device_id={"d": lax.rem(me + i, d["D"])}, device_id_type=MESH).start()
-
-    ln_all[me] = ln_ref[...]
-
-
-def spread_scale_wait(d, ln_all, ln_send, ln_recv):
-    rest = ln_all.at[pl.ds(0, d["D"] - 1)]
-    pltpu.make_async_copy(rest, rest, ln_recv).wait()
-    pltpu.make_async_copy(rest, rest, ln_send).wait()
+    for device in comm.near():
+        pl.semaphore_signal(barrier, inc=1, device_id=device, device_id_type=MESH)
+
+
+def meet(comm):
+    pl.semaphore_wait(pltpu.get_barrier_semaphore(), len(comm.near()))
+
+
+def scale_stage(comm, stage, ln_all, send, recv):
+    x, y, c = comm.x, comm.y, comm.core
+
+    def put(ref, device):
+        pltpu.make_async_remote_copy(src_ref=ref, dst_ref=ref, send_sem=send.at[stage], recv_sem=recv.at[stage],
+                                     device_id=device, device_id_type=MESH).start()
+
+    arrived = (None, ln_all.at[0, 0], ln_all.at[0, 0, 0], ln_all.at[0], ln_all.at[0, :, 0])[stage]
+    if stage:
+        pltpu.make_async_copy(arrived, arrived, recv.at[stage - 1]).wait()
+    if stage == 0:
+        for s in (1, -1):
+            put(ln_all.at[y, x, c], comm.dev(y, comm.wrap(x + s), c))
+    elif stage == 1:
+        put(ln_all.at[y, comm.wrap(x - 1), c], comm.dev(y, comm.wrap(x + 1), c))
+    elif stage == 2:
+        for s in (1, -1):
+            put(ln_all.at[y, :, c], comm.dev(comm.wrap(y + s), x, c))
+    elif stage == 3:
+        put(ln_all.at[comm.wrap(y - 1), :, c], comm.dev(comm.wrap(y + 1), x, c))
+    else:
+        put(ln_all.at[:, :, c], comm.dev(y, x, 1 - c))
+
+
+def scale_wait(ln_all, send, recv):
+    half = ln_all.at[:, :, 0]
+    pltpu.make_async_copy(half, half, recv.at[4]).wait()
+    for stage, ref in enumerate((ln_all.at[0, 0], ln_all.at[0, 0, 0], ln_all.at[0], ln_all.at[0, :, 0], half)):
+        pltpu.make_async_copy(ref, ref, send.at[stage]).wait()
 
 
 def scale_row(d, ln_all, row_ref):
     per = 128 // d["R"]
+    side, cores = d["SIDE"], d["CORES"]
     for i in range(d["E"] // 128):
-        row_ref[0:1, i * 128:(i + 1) * 128] = jnp.concatenate([ln_all[per * i + k] for k in range(per)], axis=1)
+        parts = [ln_all[n // (side * cores), n // cores % side, n % cores] for n in range(per * i, per * (i + 1))]
+        row_ref[0:1, i * 128:(i + 1) * 128] = jnp.concatenate(parts, axis=1)
 
 
 def nn(a, b):
@@ -387,7 +405,7 @@
     bf16, f32, dma = jnp.bfloat16, jnp.float32, pltpu.SemaphoreType.DMA
     return [
         pltpu.VMEM((d["R"], d["COLS"]), bf16),
-        pltpu.VMEM((d["D"], 1, d["R"]), f32),
+        pltpu.VMEM((d["SIDE"], d["SIDE"], d["CORES"], 1, d["R"]), f32),
         pltpu.VMEM((1, E), f32),
         pltpu.VMEM((T, E), bf16),
         pltpu.VMEM((T, E), f32),
@@ -403,7 +421,7 @@
         pltpu.VMEM((2, T, FC), bf16),
         pltpu.VMEM((2, 2) + unit, bf16),
         pltpu.VMEM((3,) + unit, bf16),
-        dma((4,)), dma, dma, dma((5,)), dma((5, SMALL + (d["COLS"] - SMALL * SMALL_WIDTH) // WIDTH)),
+        dma((5,)), dma((5,)), dma((5,)), dma((5,)), dma((5, SMALL + (d["COLS"] - SMALL * SMALL_WIDTH) // WIDTH)),
         dma((max(T // Layer.XB, E // FC),)), dma((2, 2)), dma((3,)), dma((2,)),
     ]
 
@@ -471,13 +489,16 @@
     own = [pltpu.make_async_copy(r.stage.at[:, part], mine.at[:, part], r.local_sem.at[2 + i])
            for i, part in enumerate((early, late))]
     rest = r.stage.at[:, late]
+    own_scale = pltpu.make_async_copy(r.ln_own, r.ln_all.at[comm.y, comm.x, comm.core], r.local_sem.at[4])
+    arrive(comm)
+    own_scale.start()
     order_copies(d, r.win, r.wot, r.stage, r.local_sem, 0)
-    arrive(d)
     for i in range(xbs):
         L.x_copy(i).start()
     pltpu.make_async_copy(r.stage.at[:, early], r.stage.at[:, early], r.local_sem.at[0]).wait()
     own[0].start()
-    meet(d)
+    own_scale.wait()
+    meet(comm)
     reached = set()
 
     def late_begun():
@@ -498,7 +519,7 @@
             reached.add("placed")
             own[1].wait()
 
-    normed = keyed = queried = 0
+    normed = keyed = queried = scaled = 0
     next_group = [0] * 6
     for what in OPENING:
         if what <= 5:
@@ -512,8 +533,6 @@
                 late_placed()
             with jax.named_scope(f"stage{what}"):
                 comm.stage_fn(what, g, g < SMALL)
-            if (what, g) == (0, 1):
-                spread_scale(d, r.ln_own, r.ln_all, r.ln_send, r.ln_recv)
             if what == 1:
                 late_begun()
             if what == 5 and comm.end(g) < 3 * HD <= comm.end(g + 1):
@@ -522,6 +541,10 @@
             if what == 5 and comm.end(g) < 5 * HD <= comm.end(g + 1):
                 start(fetch_q(1))
                 start(fetch_o(0))
+        elif what == SCALE:
+            with jax.named_scope("scale"):
+                scale_stage(comm, scaled, r.ln_all, r.ln_send, r.ln_recv)
+            scaled += 1
         elif what == KEYS:
             if keyed == 0:
                 assert normed == xbs
@@ -548,7 +571,7 @@
                     L.tables()
                     L.bias()
                 with jax.named_scope("wait_scale"):
-                    spread_scale_wait(d, r.ln_all, r.ln_send, r.ln_recv)
+                    scale_wait(r.ln_all, r.ln_send, r.ln_recv)
                     scale_row(d, r.ln_all, r.ln)
             many = min(what - NORM, xbs - normed)
             if many > 0:
@@ -659,7 +682,7 @@
         functools.partial(kernel, d),
         out_shape=(jax.ShapeDtypeStruct(x.shape, jnp.bfloat16), cache, cache,
                    jax.ShapeDtypeStruct(w_shape, jnp.bfloat16)),
-        in_specs=[vmem, hbm, hbm, hbm, pl.BlockSpec(memory_space=pltpu.SMEM), vmem, vmem],
+        in_specs=[hbm, hbm, hbm, hbm, pl.BlockSpec(memory_space=pltpu.SMEM), vmem, vmem],
         out_specs=(hbm, hbm, hbm, hbm),
         scratch_shapes=scratch(d),
         compiler_params=pltpu.CompilerParams(collective_id=0, has_side_effects=True, vmem_limit_bytes=VMEM_LIMIT),

time: 370 us -> 375 us (1.014)
  Pallas kernels: 369 us -> 373 us
    pallas_call x1, Pallas kernels: 361 us -> 364 us  [layer(): pl.pallas_call(functools.partial(kernel, d), out_shape=(jax.ShapeDtypeStr...]
where the time goes in v7:
time: 375 us; the launch traced here: 374 us
  Pallas kernels  373 us (99%)
    pallas_call x1, Pallas kernels, layer(): pl.pallas_call(functools.partial(kernel, d), out_shape=(jax.ShapeDtypeStr...  364 us
    pallas_call x1, Pallas kernels, hand_on(): pl.pallas_call(functools.partial(hand_on_kernel, parts), out_shape=tuple(...  8.19 us

profile of v7, /device:TPU:96, one launch (start us, length us, event | category | flops | bytes accessed | tf_op | source)
XLA Modules:
  0.0 374.0 jit_solution(5332231912569707199)
XLA Ops:
  1.3 364.3 %layer.1 = (bf16[1,2048,2048]{2,1,0:T(8,128)(2,1)}, bf16[1,2048,256]{2,1,0:T(8,128)(2,1)}, bf16[1,2048,256]{2,1,0:T(8,128)(2,1)}, bf16[4,4,2,64,29184]{4,3,2,1,0:T(8,128)(2,1)}) custom-call(f32[1,64]{1,0:T(1,128)} %bitcast.3, bf16[64,18944]{1,0:T(8,128)(2,1)} %refs_1_.1, bf16[64,10240]{1,0:T(8,128)(2,1)} %bitcast.2, bf16[1,2048,2048]{2,1,0:T(8,128)(2,1)} %refs_3_.1, ...), custom_call_target="tpu_custom_call" | custom-call | flops 261993005056 | bytes 136314880 | tf_op jit(solution)/shard_map/layer/pallas_call | solution.py:681
  365.6 8.2 %hand_on.1 = (bf16[1,2048,2048]{2,1,0:T(8,128)(2,1)}, bf16[1,2048,256]{2,1,0:T(8,128)(2,1)}, bf16[1,2048,256]{2,1,0:T(8,128)(2,1)}) custom-call(bf16[1,2048,2048]{2,1,0:T(8,128)(2,1)} %get-tuple-element.6.refs_0_, bf16[1,2048,256]{2,1,0:T(8,128)(2,1)} %get-tuple-element.7.refs_1_, bf16[1,2048,256]{2,1,0:T(8,128)(2,1)} %get-tuple-element.8.refs_2_), custom_call_target="tpu_custom_call" | custom-call | tf_op jit(solution)/shard_map/hand_on/pallas_call | solution.py:716
